TPU v7x, 64 devices: a 2x2x8 block of a 4x4x8 slice. The times are simulated.
64 devices in a mesh: dp: 4 (over x, y), tp: 16 (over z, core).
Axes of the slice: x: 2, y: 2, z: 8, core: 2. Of those that a mesh axis runs over, the one named last changes fastest.
The devices are a block of a 4x4x8 slice.
Arguments:
- hidden: bfloat16 [128, 3, 4096], P('dp'), parts along dimension 0
- draft_ids: int32 [128, 2], P('dp'), parts along dimension 0
- norm_gain: bfloat16 [4096], replicated
- head_w: bfloat16 [4096, 32000], P(None, 'tp')
Outputs:
- output 1: float32 [128, 2], P('dp'), parts along dimension 0
- output 2: float32 [128, 3], P('dp'), parts along dimension 0
- output 3: float32 [128, 3], P('dp'), parts along dimension 0
There are 4 independent parts. A program takes and returns all parts, laid end to end along the dimension named above; an argument that names none is the same for every part.
All inputs are finite; a program needn't handle non-finite values.
Results may differ from a plain program's by a relative error of at most 0.001.
Values sent between devices are 32-bit elements.
A program may use at most 768 MiB of HBM per device.

v0:
```python
import jax
import jax.numpy as jnp
from jax import lax
from jax.sharding import PartitionSpec as P

NORM_EPS = 1e-5


def rms_norm(hidden, norm_gain):
    wide_x = hidden.astype(jnp.float32)
    inv_rms = lax.rsqrt(jnp.mean(wide_x * wide_x, axis=-1, keepdims=True) + NORM_EPS)
    return (wide_x * inv_rms * norm_gain.astype(jnp.float32)).astype(jnp.bfloat16)


def solution(mesh):
    def per_device(hidden, draft_ids, norm_gain, head_w):
        normed = rms_norm(hidden, norm_gain)
        logits = jnp.einsum('btd,dv->btv', normed, head_w, preferred_element_type=jnp.float32)
        gathered = lax.all_gather(logits, 'tp')
        shards = gathered.shape[0]
        shard_cols = gathered.shape[3]
        drafts = draft_ids.shape[1]
        row_max = jnp.max(gathered, axis=(0, 3))
        shifted = gathered - row_max[None, :, :, None]
        exp_vals = jnp.exp(shifted)
        exp_sum = jnp.sum(exp_vals, axis=(0, 3))
        weighted = jnp.sum(exp_vals * shifted, axis=(0, 3))
        log_sum = jnp.log(exp_sum)
        log_norm = row_max + log_sum
        entropy = log_sum - weighted / exp_sum
        col_ids = lax.broadcasted_iota(jnp.int32, (shards, 1, 1, shard_cols), 0) * shard_cols + lax.broadcasted_iota(jnp.int32, (shards, 1, 1, shard_cols), 3)
        picked = jnp.sum(jnp.where(col_ids == draft_ids[None, :, :, None], gathered[:, :, :drafts], 0.0), axis=(0, 3))
        return picked - log_norm[:, :drafts], log_norm, entropy

    specs_in = (P('dp', None, None), P('dp', None), P(None), P(None, 'tp'))
    specs_out = (P('dp', None), P('dp', None), P('dp', None))
    return jax.shard_map(per_device, mesh=mesh, in_specs=specs_in, out_specs=specs_out, check_vma=False)
```

profile of v0, /device:TPU:21, one launch (start us, length us, event | category | flops | bytes accessed | tf_op | source)
XLA Modules:
  0.0 122.9 jit_solution(12695698291735671287)
XLA Ops:
  7.2 0.1 all-gather.3.cloned.1.call-start
  7.2 0.7 convert_element_type.10
  7.9 1.4 %fusion.4 = f32[32,3]{0,1:T(4,128)S(1)} fusion(bf16[32,3,4096]{2,0,1:T(8,128)(2,1)} %param.4), kind=kLoop, calls=%fused_computation.9 | loop fusion | flops 1179552 | bytes 786816 | tf_op jit(solution)/shard_map/reduce_sum | solution.py:11
  9.3 12.0 %fusion = f32[32,3,2000]{2,0,1:T(8,128)} fusion(bf16[4096,2000]{0,1:T(8,128)(2,1)} %param.7, bf16[32,3,4096]{2,0,1:T(8,128)(2,1)} %param.4, f32[4096]{0:T(1024)S(1)} %convert_element_type.10, f32[32,3]{0,1:T(4,128)S(1)} %add_rsqrt_fusion), kind=kOutput, calls=%fused_computation.2 | convolution fusion | flops 1574436864 | bytes 17955200 | tf_op jit(solution)/shard_map/btd,dv->btv/dot_general | solution.py:18
  21.3 0.1 all-gather.3.cloned.1.call-update
  21.4 0.1 iota_add_fusion
  21.5 77.3 %all-gather.3.cloned.1.call-done = f32[512,3,2000]{2,0,1:T(8,128)} async-done(((f32[32,3,2000]{2,0,1:T(8,128)}), f32[512,3,2000]{2,0,1:T(8,128)}) %all-gather.3.cloned.1.call-update) | async-done | bytes 12288016 | tf_op jit(solution)/shard_map/all_gather | solution.py:19
  98.8 5.2 %reduce = f32[512,3]{0,1:T(4,128)S(1)} reduce(f32[512,3,2000]{2,0,1:T(8,128)} %all-gather.3.cloned.1.call-done, f32[]{:T(128)} %constant.10.clone.1), dimensions={2}, to_apply=%region_2.0 | reduce | flops 3070464 | bytes 12294148 | tf_op jit(solution)/shard_map/reduce_max | solution.py:23
  104.0 0.0 copy-start.2
  104.0 0.1 reshape.32
  104.1 0.0 copy-start
  104.1 8.7 %fusion.2 = (f32[32,3]{0,1:T(4,128)S(1)}, f32[32,3]{0,1:T(4,128)S(1)}) fusion(f32[16,32,3,2000]{3,1,0,2:T(8,128)} %bitcast.6, f32[32,3]{0,1:T(4,128)S(1)} %reduce_max.9), kind=kLoop, calls=%fused_computation.4 | loop fusion | flops 12287808 | bytes 12289152 | tf_op jit(solution)/shard_map/reduce_sum | solution.py:27
  112.8 0.6 divide_subtract_fusion
  113.4 0.0 copy-done.2
  113.4 0.0 copy-done
  113.4 0.0 copy-start.1
  113.4 2.0 %fusion.3 = f32[32,2]{0,1:T(2,128)S(1)} fusion(f32[16,32,3,2000]{3,1,0,2:T(8,128)S(1)} %bitcast.7, s32[32,2]{0,1:T(2,128)S(1)} %copy-done.2, s32[16,2000]{1,0:T(8,128)S(1)} %iota_add_fusion), kind=kLoop, calls=%fused_computation.6 | loop fusion | flops 6143936 | bytes 8320512 | tf_op jit(solution)/shard_map/reduce_sum | solution.py:32
  115.4 0.6 slice_subtract_fusion
  116.0 0.0 copy-done.1
  (3 shorter events, 0.0 us)
Async XLA Ops:
  7.2 91.6 %all-gather.3.cloned.1.call-start = ((), (), s32[]{:S(2)}) async-start(), calls=%async_computation | async-start | bytes 13369344 | tf_op jit(solution)/shard_map/all_gather | solution.py:19
  104.0 9.4 %copy-start.2 = (s32[32,2]{0,1:T(2,128)S(1)}, s32[32,2]{0,1:T(2,128)}, u32[]{:S(2)}) copy-start(s32[32,2]{0,1:T(2,128)} %param.5) | copy-start | bytes 772
  104.1 9.3 %copy-start = (f32[512,3,2000]{2,0,1:T(8,128)S(1)}, f32[512,3,2000]{2,0,1:T(8,128)}, u32[]{:S(2)}) copy-start(f32[512,3,2000]{2,0,1:T(8,128)} %all-gather.3.cloned.1.call-done) | copy-start | bytes 36864004
  113.4 2.6 %copy-start.1 = (f32[32,3]{0,1:T(4,128)}, f32[32,3]{0,1:T(4,128)S(1)}, u32[]{:S(2)}) copy-start(f32[32,3]{0,1:T(4,128)S(1)} %get-tuple-element.6) | copy-start | bytes 1156
Sparse Core Ops, SparseCore 0:
  21.5 77.2 all-gather.2
where the time goes:
time: 123 us
  waiting for transfers between devices  77.4 us (63%)
  other arithmetic  19.3 us (16%)
  between operations  14.1 us (11%)
  matrix products  12 us (10%)
    all_gather x1, waiting for transfers between devices, per_device(): gathered = lax.all_gather(logits, 'tp')  77.3 us
    dot_general x1, matrix products, per_device(): jnp.einsum('btd,dv->btv', normed, head_w, preferred_element_type=jnp.floa...  12 us
    reduce_sum x1, other arithmetic, per_device(): weighted = jnp.sum(exp_vals * shifted, axis=(0, 3))  8.68 us
    reduce_max x2, other arithmetic, per_device(): row_max = jnp.max(gathered, axis=(0, 3))  5.23 us
  transfers between devices with their start and end apart: 1, of which 1 were waited for; matrix products, arithmetic and copies ran while one was open for 0% of the time, Pallas kernels for 0%

commit v1 on v0

v1 whole, which is shorter than its diff:
```python
import functools

import jax
import jax.numpy as jnp
from jax import lax
from jax.experimental import pallas as pl
from jax.experimental.pallas import tpu as pltpu
from jax.sharding import PartitionSpec as P

NORM_EPS = 1e-5
LANES = 128
SUBLANES = 8


def chunk_bounds(total):
    step = 256
    return [(start, min(step, total - start)) for start in range(0, total, step)]


def head_kernel(
    peers,
    x_hbm, ids_ref, gain_ref, w_hbm,
    logp_ref, norm_ref, ent_ref,
    x_vmem, n_vmem, w_vmem, own, recv,
    x_sem, w_sem, send_sem, recv_sem,
):
    steps, seqs, dim = x_vmem.shape
    rows = steps * seqs
    drafts = ids_ref.shape[0]
    cols = w_vmem.shape[0]
    chunks = chunk_bounds(cols)
    me = lax.axis_index('tp')

    x_copies = [pltpu.make_async_copy(x_hbm.at[t], x_vmem.at[t], x_sem.at[t]) for t in range(steps)]
    w_copies = [
        pltpu.make_async_copy(w_hbm.at[pl.ds(start, size)], w_vmem.at[pl.ds(start, size)], w_sem.at[i])
        for i, (start, size) in enumerate(chunks)
    ]
    for copy in x_copies + w_copies:
        copy.start()

    barrier = pltpu.get_barrier_semaphore()
    for hop in range(1, peers):
        pl.semaphore_signal(
            barrier, inc=1, device_id={'tp': lax.rem(me + hop, peers)}, device_id_type=pl.DeviceIdType.MESH
        )

    ids = jnp.concatenate(
        [ids_ref[pl.ds(t, 1), :] for t in range(drafts)] + [jnp.full((1, rows - drafts * seqs), -1, jnp.int32)], axis=1
    )
    local_ids = ids - me * cols

    gain = gain_ref[...].astype(jnp.float32)
    for t in range(steps):
        x_copies[t].wait()
        wide_x = x_vmem[t].astype(jnp.float32)
        inv_rms = lax.rsqrt(jnp.mean(wide_x * wide_x, axis=-1, keepdims=True) + NORM_EPS)
        n_vmem[pl.ds(t * seqs, seqs), :] = (wide_x * inv_rms * gain).astype(jnp.bfloat16)

    groups = (SUBLANES, rows)
    top = exp_sum = weighted = picked = None
    for i, (start, size) in enumerate(chunks):
        w_copies[i].wait()
        logits = lax.dot_general(
            w_vmem[pl.ds(start, size), :], n_vmem[...], (((1,), (1,)), ((), ())),
            preferred_element_type=jnp.float32,
        )
        tiles = logits.reshape(size // SUBLANES, SUBLANES, rows)
        col_ids = lax.broadcasted_iota(jnp.int32, tiles.shape, 0) * SUBLANES + (
            lax.broadcasted_iota(jnp.int32, tiles.shape, 1) + start
        )
        hit = jnp.sum(jnp.where(col_ids == local_ids[None], tiles, 0.0), axis=0)
        chunk_top = jnp.max(tiles, axis=0)
        new_top = chunk_top if top is None else jnp.maximum(top, chunk_top)
        shifted = tiles - new_top[None]
        exp_vals = jnp.exp(shifted)
        chunk_sum = jnp.sum(exp_vals, axis=0)
        chunk_weighted = jnp.sum(exp_vals * shifted, axis=0)
        if top is None:
            exp_sum, weighted, picked = chunk_sum, chunk_weighted, hit
        else:
            drop = top - new_top
            scale = jnp.exp(drop)
            weighted = chunk_weighted + scale * (weighted + exp_sum * drop)
            exp_sum = chunk_sum + scale * exp_sum
            picked = picked + hit
        top = new_top

    all_top = jnp.max(top, axis=0, keepdims=True)
    drop = top - all_top
    scale = jnp.exp(drop)
    own_sum = jnp.sum(scale * exp_sum, axis=0, keepdims=True)
    own_weighted = jnp.sum(scale * (weighted + exp_sum * drop), axis=0, keepdims=True)
    own_picked = jnp.sum(picked, axis=0, keepdims=True)
    stats = jnp.concatenate([all_top, own_sum, own_weighted, own_picked], axis=0)
    stats = jnp.concatenate([stats, jnp.zeros((stats.shape[0], LANES - rows), jnp.float32)], axis=1)
    own[...] = stats
    recv[me] = stats

    pl.semaphore_wait(barrier, peers - 1)
    for hop in range(1, peers):
        pltpu.make_async_remote_copy(
            src_ref=own, dst_ref=recv.at[me], send_sem=send_sem, recv_sem=recv_sem,
            device_id={'tp': lax.rem(me + hop, peers)}, device_id_type=pl.DeviceIdType.MESH,
        ).start()
    others = recv.at[pl.ds(0, peers - 1)]
    pltpu.make_async_copy(others, others, recv_sem).wait()

    parts = recv[...]
    tops = parts[:, 0:1, :rows]
    full_top = jnp.max(tops, axis=0)
    drop = tops - full_top[None]
    scale = jnp.exp(drop)
    sums = parts[:, 1:2, :rows]
    full_sum = jnp.sum(scale * sums, axis=0)
    full_weighted = jnp.sum(scale * (parts[:, 2:3, :rows] + sums * drop), axis=0)
    full_picked = jnp.sum(parts[:, 3:4, :rows], axis=0)
    log_sum = jnp.log(full_sum)
    log_norm = full_top + log_sum
    entropy = log_sum - full_weighted / full_sum
    logp = full_picked - log_norm
    for t in range(steps):
        lanes = slice(t * seqs, (t + 1) * seqs)
        norm_ref[pl.ds(t, 1), :] = log_norm[:, lanes]
        ent_ref[pl.ds(t, 1), :] = entropy[:, lanes]
        if t < drafts:
            logp_ref[pl.ds(t, 1), :] = logp[:, lanes]
    pltpu.make_async_copy(others, others, send_sem).wait()


def solution(mesh):
    peers = mesh.shape['tp']

    def per_device(hidden, draft_ids, norm_gain, head_w):
        seqs, steps, dim = hidden.shape
        drafts = draft_ids.shape[1]
        cols = head_w.shape[1]
        rows = steps * seqs
        chunks = chunk_bounds(cols)
        vmem = pl.BlockSpec(memory_space=pltpu.VMEM)
        anywhere = pl.BlockSpec(memory_space=pl.ANY)
        logp, log_norm, entropy = pl.pallas_call(
            functools.partial(head_kernel, peers),
            out_shape=(
                jax.ShapeDtypeStruct((drafts, seqs), jnp.float32),
                jax.ShapeDtypeStruct((steps, seqs), jnp.float32),
                jax.ShapeDtypeStruct((steps, seqs), jnp.float32),
            ),
            in_specs=[anywhere, vmem, vmem, anywhere],
            out_specs=(vmem, vmem, vmem),
            scratch_shapes=[
                pltpu.VMEM((steps, seqs, dim), jnp.bfloat16),
                pltpu.VMEM((rows, dim), jnp.bfloat16),
                pltpu.VMEM((cols, dim), jnp.bfloat16),
                pltpu.VMEM((4, LANES), jnp.float32),
                pltpu.VMEM((peers, 4, LANES), jnp.float32),
                pltpu.SemaphoreType.DMA((steps,)),
                pltpu.SemaphoreType.DMA((len(chunks),)),
                pltpu.SemaphoreType.DMA,
                pltpu.SemaphoreType.DMA,
            ],
            compiler_params=pltpu.CompilerParams(
                collective_id=0, has_side_effects=True, vmem_limit_bytes=60 * 1024 * 1024
            ),
        )(hidden.transpose(1, 0, 2), draft_ids.T, norm_gain.reshape(1, dim), head_w.T)
        return logp.T, log_norm.T, entropy.T

    specs_in = (P('dp', None, None), P('dp', None), P(None), P(None, 'tp'))
    specs_out = (P('dp', None), P('dp', None), P('dp', None))
    return jax.shard_map(per_device, mesh=mesh, in_specs=specs_in, out_specs=specs_out, check_vma=False)
```

time: 123 us -> 33.6 us (0.27)
  waiting for transfers between devices: 77.4 us -> 0 us
  Pallas kernels: 0 us -> 27.7 us
  other arithmetic: 19.3 us -> 0 us
  between operations: 14.1 us -> 0.64 us
  matrix products: 12 us -> 0 us
  local copies, waits for them, and re-layouts: 0.09 us -> 4.98 us
    all_gather x1 -> x0, waiting for transfers between devices: 77.3 us -> none  [per_device(): gathered = lax.all_gather(logits, 'tp')]
    pallas_call x0 -> x1, Pallas kernels: none -> 27.7 us  [per_device(): pl.pallas_call(functools.partial(head_kernel, peers), out_shape=(jax.Shap...]
    reduce_sum x3 -> x0, other arithmetic: 12.1 us -> none  [the longest x1 8.68 us: per_device(): weighted = jnp.sum(exp_vals * shifted, axis=(0, 3))]
    dot_general x1 -> x0, matrix products: 12 us -> none  [per_device(): jnp.einsum('btd,dv->btv', normed, head_w, preferred_element_type=jnp.floa...]
    reduce_max x2 -> x0, other arithmetic: 5.23 us -> none  [per_device(): row_max = jnp.max(gathered, axis=(0, 3))]
    unnamed x6 -> x3, local copies, waits for them, and re-layouts: 0.01 us -> 3.67 us
    reshape x0 -> x1, local copies, waits for them, and re-layouts: none -> 1.31 us  [per_device(): norm_gain.reshape(1, dim)]
  transfers between devices with their start and end apart: 1 -> 0, of which waited for: 1 -> 0; matrix products, arithmetic and copies ran while one was open for 0% -> 0% of each run, Pallas kernels for 0% -> 0%
where the time goes in v1:
time: 33.6 us; the launch traced here: 33.3 us
  Pallas kernels  27.7 us (82%)
  local copies, waits for them, and re-layouts  4.98 us (15%)
  between operations  0.64 us (2%)
    pallas_call x1, Pallas kernels, per_device(): pl.pallas_call(functools.partial(head_kernel, peers), out_shape=(jax.Shap...  27.7 us
    unnamed x3, local copies, waits for them, and re-layouts  3.67 us
    reshape x1, local copies, waits for them, and re-layouts, per_device(): norm_gain.reshape(1, dim)  1.31 us

profile of v1, /device:TPU:21, one launch (start us, length us, event | category | flops | bytes accessed | tf_op | source)
XLA Modules:
  0.0 33.3 jit_solution(12194172699917178159)
XLA Ops:
  0.6 1.3 %reshape.9.gain_ref = bf16[1,4096]{1,0:T(2,128)(2,1)} reshape(bf16[4096]{0:T(1024)(128)(2,1)} %param.6) | data formatting | bytes 16384 | tf_op jit(solution)/shard_map/reshape | solution.py:165
  1.9 27.7 %shard_map.67 = (f32[2,32]{1,0:T(2,128)}, f32[3,32]{1,0:T(4,128)}, f32[3,32]{1,0:T(4,128)}) custom-call(bf16[3,32,4096]{2,1,0:T(8,128)(2,1)} %bitcast.7, s32[2,32]{1,0:T(2,128)} %bitcast.10, bf16[1,4096]{1,0:T(2,128)(2,1)} %reshape.9.gain_ref, bf16[2000,4096]{1,0:T(8,128)(2,1)} %bitcast.6), custom_call_target="tpu_custom_call" | custom-call | tf_op jit(solution)/shard_map/pallas_call | solution.py:142
  29.6 1.2 %copy.10 = f32[32,2]{0,1:T(2,128)} copy(f32[32,2]{0,1:T(2,128)} %bitcast.11) | data formatting | bytes 512
  30.8 1.2 %copy.11 = f32[32,3]{0,1:T(4,128)} copy(f32[32,3]{0,1:T(4,128)} %bitcast.9) | data formatting | bytes 768
  32.1 1.2 %copy.12 = f32[32,3]{0,1:T(4,128)} copy(f32[32,3]{0,1:T(4,128)} %bitcast.8) | data formatting | bytes 768

commit v2 on v1

--- a/solution.py
+++ b/solution.py
@@ -10,33 +10,38 @@
 NORM_EPS = 1e-5
 LANES = 128
 SUBLANES = 8
+TILE = 256
+STEP_ROWS = 400
 
 
 def chunk_bounds(total):
-    step = 256
-    return [(start, min(step, total - start)) for start in range(0, total, step)]
+    return [(start, min(STEP_ROWS, total - start)) for start in range(0, total, STEP_ROWS)]
 
 
 def head_kernel(
     peers,
-    x_hbm, ids_ref, gain_ref, w_hbm,
+    x_hbm, ids_hbm, gain_hbm, w_hbm,
     logp_ref, norm_ref, ent_ref,
-    x_vmem, n_vmem, w_vmem, own, recv,
-    x_sem, w_sem, send_sem, recv_sem,
+    x_vmem, ids_vmem, gain_vmem, n_vmem, w_vmem, z_vmem, own, recv,
+    x_sem, small_sem, w_sem, send_sem, recv_sem,
 ):
     steps, seqs, dim = x_vmem.shape
     rows = steps * seqs
-    drafts = ids_ref.shape[0]
+    drafts = ids_vmem.shape[0]
     cols = w_vmem.shape[0]
     chunks = chunk_bounds(cols)
     me = lax.axis_index('tp')
 
+    ids_copy = pltpu.make_async_copy(ids_hbm, ids_vmem, small_sem.at[0])
+    gain_copy = pltpu.make_async_copy(gain_hbm, gain_vmem, small_sem.at[1])
     x_copies = [pltpu.make_async_copy(x_hbm.at[t], x_vmem.at[t], x_sem.at[t]) for t in range(steps)]
     w_copies = [
         pltpu.make_async_copy(w_hbm.at[pl.ds(start, size)], w_vmem.at[pl.ds(start, size)], w_sem.at[i])
         for i, (start, size) in enumerate(chunks)
     ]
-    for copy in x_copies + w_copies:
+    for copy in x_copies + [gain_copy, ids_copy]:
+        copy.start()
+    for copy in w_copies:
         copy.start()
 
     barrier = pltpu.get_barrier_semaphore()
@@ -45,27 +50,30 @@
             barrier, inc=1, device_id={'tp': lax.rem(me + hop, peers)}, device_id_type=pl.DeviceIdType.MESH
         )
 
+    for t in range(steps):
+        x_copies[t].wait()
+        if t == 0:
+            gain_copy.wait()
+        wide = [x_vmem[t, :, pl.ds(c, LANES)].astype(jnp.float32) for c in range(0, dim, LANES)]
+        squares = [x * x for x in wide]
+        while len(squares) > 1:
+            squares = [a + b for a, b in zip(squares[::2], squares[1::2])]
+        mean = jnp.sum(squares[0], axis=-1, keepdims=True) / dim
+        inv_rms = lax.rsqrt(mean + NORM_EPS)
+        for c, x in enumerate(wide):
+            gain = gain_vmem[pl.ds(c, 1), :].astype(jnp.float32)
+            n_vmem[pl.ds(t * seqs, seqs), pl.ds(c * LANES, LANES)] = (x * inv_rms * gain).astype(jnp.bfloat16)
+
+    ids_copy.wait()
     ids = jnp.concatenate(
-        [ids_ref[pl.ds(t, 1), :] for t in range(drafts)] + [jnp.full((1, rows - drafts * seqs), -1, jnp.int32)], axis=1
+        [ids_vmem[pl.ds(t, 1), :] for t in range(drafts)] + [jnp.full((1, rows - drafts * seqs), -1, jnp.int32)],
+        axis=1,
     )
     local_ids = ids - me * cols
 
-    gain = gain_ref[...].astype(jnp.float32)
-    for t in range(steps):
-        x_copies[t].wait()
-        wide_x = x_vmem[t].astype(jnp.float32)
-        inv_rms = lax.rsqrt(jnp.mean(wide_x * wide_x, axis=-1, keepdims=True) + NORM_EPS)
-        n_vmem[pl.ds(t * seqs, seqs), :] = (wide_x * inv_rms * gain).astype(jnp.bfloat16)
-
-    groups = (SUBLANES, rows)
-    top = exp_sum = weighted = picked = None
-    for i, (start, size) in enumerate(chunks):
-        w_copies[i].wait()
-        logits = lax.dot_general(
-            w_vmem[pl.ds(start, size), :], n_vmem[...], (((1,), (1,)), ((), ())),
-            preferred_element_type=jnp.float32,
-        )
-        tiles = logits.reshape(size // SUBLANES, SUBLANES, rows)
+    def stats_of(carry, start, size, tiles):
+        top, exp_sum, weighted, picked = carry
+        tiles = tiles.reshape(size // SUBLANES, SUBLANES, rows)
         col_ids = lax.broadcasted_iota(jnp.int32, tiles.shape, 0) * SUBLANES + (
             lax.broadcasted_iota(jnp.int32, tiles.shape, 1) + start
         )
@@ -77,25 +85,54 @@
         chunk_sum = jnp.sum(exp_vals, axis=0)
         chunk_weighted = jnp.sum(exp_vals * shifted, axis=0)
         if top is None:
-            exp_sum, weighted, picked = chunk_sum, chunk_weighted, hit
-        else:
-            drop = top - new_top
-            scale = jnp.exp(drop)
-            weighted = chunk_weighted + scale * (weighted + exp_sum * drop)
-            exp_sum = chunk_sum + scale * exp_sum
-            picked = picked + hit
-        top = new_top
-
-    all_top = jnp.max(top, axis=0, keepdims=True)
-    drop = top - all_top
-    scale = jnp.exp(drop)
-    own_sum = jnp.sum(scale * exp_sum, axis=0, keepdims=True)
-    own_weighted = jnp.sum(scale * (weighted + exp_sum * drop), axis=0, keepdims=True)
-    own_picked = jnp.sum(picked, axis=0, keepdims=True)
-    stats = jnp.concatenate([all_top, own_sum, own_weighted, own_picked], axis=0)
-    stats = jnp.concatenate([stats, jnp.zeros((stats.shape[0], LANES - rows), jnp.float32)], axis=1)
-    own[...] = stats
-    recv[me] = stats
+            return new_top, chunk_sum, chunk_weighted, hit
+        drop = top - new_top
+        scale = jnp.exp(drop)
+        return (
+            new_top,
+            chunk_sum + scale * exp_sum,
+            chunk_weighted + scale * (weighted + exp_sum * drop),
+            picked + hit,
+        )
+
+    halves = 2
+    per_half = dim // TILE // halves
+
+    def run(accs):
+        carry = (None,) * 4
+
+        def drain(i, carry):
+            start, size = chunks[i]
+            low, high = (pltpu.matmul_pop(acc)[:, :LANES] for acc in accs[i % 2])
+            return stats_of(carry, start, size, low + high)
+
+        pending = None
+        for i, (start, size) in enumerate(chunks):
+            w_copies[i].wait()
+            outs = []
+            part = size // 2
+            for half in range(2):
+                outs.append(lax.dot_general(w_vmem[pl.ds(start + half * part, part), :], n_vmem[...], (((1,), (1,)), ((), ())), preferred_element_type=jnp.float32))
+            if pending is not None:
+                carry = stats_of(carry, *pending)
+            pending = (start, size, jnp.concatenate(outs, axis=0))
+        return stats_of(carry, *pending)
+
+    def body(*refs):
+        top, exp_sum, weighted, picked = run(None)
+
+        all_top = jnp.max(top, axis=0, keepdims=True)
+        drop = top - all_top
+        scale = jnp.exp(drop)
+        own_sum = jnp.sum(scale * exp_sum, axis=0, keepdims=True)
+        own_weighted = jnp.sum(scale * (weighted + exp_sum * drop), axis=0, keepdims=True)
+        own_picked = jnp.sum(picked, axis=0, keepdims=True)
+        stats = jnp.concatenate([all_top, own_sum, own_weighted, own_picked], axis=0)
+        stats = jnp.concatenate([stats, jnp.zeros((4, LANES - rows), jnp.float32)], axis=1)
+        own[...] = stats
+        recv[me] = stats
+
+    body()
 
     pl.semaphore_wait(barrier, peers - 1)
     for hop in range(1, peers):
@@ -146,15 +183,19 @@
                 jax.ShapeDtypeStruct((steps, seqs), jnp.float32),
                 jax.ShapeDtypeStruct((steps, seqs), jnp.float32),
             ),
-            in_specs=[anywhere, vmem, vmem, anywhere],
+            in_specs=[anywhere] * 4,
             out_specs=(vmem, vmem, vmem),
             scratch_shapes=[
                 pltpu.VMEM((steps, seqs, dim), jnp.bfloat16),
+                pltpu.VMEM((drafts, seqs), jnp.int32),
+                pltpu.VMEM((dim // LANES, LANES), jnp.bfloat16),
                 pltpu.VMEM((rows, dim), jnp.bfloat16),
                 pltpu.VMEM((cols, dim), jnp.bfloat16),
+                pltpu.VMEM((STEP_ROWS, LANES), jnp.float32),
                 pltpu.VMEM((4, LANES), jnp.float32),
                 pltpu.VMEM((peers, 4, LANES), jnp.float32),
                 pltpu.SemaphoreType.DMA((steps,)),
+                pltpu.SemaphoreType.DMA((2,)),
                 pltpu.SemaphoreType.DMA((len(chunks),)),
                 pltpu.SemaphoreType.DMA,
                 pltpu.SemaphoreType.DMA,
@@ -162,7 +203,7 @@
             compiler_params=pltpu.CompilerParams(
                 collective_id=0, has_side_effects=True, vmem_limit_bytes=60 * 1024 * 1024
             ),
-        )(hidden.transpose(1, 0, 2), draft_ids.T, norm_gain.reshape(1, dim), head_w.T)
+        )(hidden.transpose(1, 0, 2), draft_ids.T, norm_gain.reshape(dim // LANES, LANES), head_w.T)
         return logp.T, log_norm.T, entropy.T
 
     specs_in = (P('dp', None, None), P('dp', None), P(None), P(None, 'tp'))

time: 33.6 us -> 26.5 us (0.79)
  Pallas kernels: 27.7 us -> 22 us
  local copies, waits for them, and re-layouts: 4.98 us -> 3.71 us
    pallas_call x1, Pallas kernels: 27.7 us -> 22 us  [per_device(): pl.pallas_call(functools.partial(head_kernel, peers), out_shape=(jax.Shap...]
    reshape x1 -> x0, local copies, waits for them, and re-layouts: 1.31 us -> none  [per_device(): norm_gain.reshape(1, dim)]
where the time goes in v2:
time: 26.5 us; the launch traced here: 26.4 us
  Pallas kernels  22 us (83%)
  local copies, waits for them, and re-layouts  3.71 us (14%)
  between operations  0.64 us (2%)
    pallas_call x1, Pallas kernels, per_device(): pl.pallas_call(functools.partial(head_kernel, peers), out_shape=(jax.Shap...  22 us
    unnamed x3, local copies, waits for them, and re-layouts  3.71 us

profile of v2, /device:TPU:21, one launch (start us, length us, event | category | flops | bytes accessed | tf_op | source)
XLA Modules:
  0.0 26.4 jit_solution(17947440789614624068)
XLA Ops:
  0.6 22.0 %shard_map.67 = (f32[2,32]{1,0:T(2,128)}, f32[3,32]{1,0:T(4,128)}, f32[3,32]{1,0:T(4,128)}) custom-call(bf16[3,32,4096]{2,1,0:T(8,128)(2,1)} %bitcast.8, s32[2,32]{1,0:T(2,128)} %bitcast.12, bf16[32,128]{1,0:T(8,128)(2,1)} %bitcast.9, bf16[2000,4096]{1,0:T(8,128)(2,1)} %bitcast.7), custom_call_target="tpu_custom_call" | custom-call | tf_op jit(solution)/shard_map/pallas_call | solution.py:179
  22.7 1.2 %copy.10 = f32[32,2]{0,1:T(2,128)} copy(f32[32,2]{0,1:T(2,128)} %bitcast.13) | data formatting | bytes 512
  23.9 1.2 %copy.11 = f32[32,3]{0,1:T(4,128)} copy(f32[32,3]{0,1:T(4,128)} %bitcast.11) | data formatting | bytes 768
  25.2 1.2 %copy.12 = f32[32,3]{0,1:T(4,128)} copy(f32[32,3]{0,1:T(4,128)} %bitcast.10) | data formatting | bytes 768

commit v3 on v2

--- a/solution.py
+++ b/solution.py
@@ -165,6 +165,15 @@
     pltpu.make_async_copy(others, others, send_sem).wait()
 
 
+def store_kernel(*refs):
+    count = (len(refs) - 1) // 2
+    copies = [pltpu.make_async_copy(refs[i], refs[count + i], refs[-1].at[i]) for i in range(count)]
+    for copy in copies:
+        copy.start()
+    for copy in copies:
+        copy.wait()
+
+
 def solution(mesh):
     peers = mesh.shape['tp']
 
@@ -176,12 +185,12 @@
         chunks = chunk_bounds(cols)
         vmem = pl.BlockSpec(memory_space=pltpu.VMEM)
         anywhere = pl.BlockSpec(memory_space=pl.ANY)
-        logp, log_norm, entropy = pl.pallas_call(
+        results = pl.pallas_call(
             functools.partial(head_kernel, peers),
             out_shape=(
-                jax.ShapeDtypeStruct((drafts, seqs), jnp.float32),
-                jax.ShapeDtypeStruct((steps, seqs), jnp.float32),
-                jax.ShapeDtypeStruct((steps, seqs), jnp.float32),
+                pltpu.VMEM((drafts, seqs), jnp.float32),
+                pltpu.VMEM((steps, seqs), jnp.float32),
+                pltpu.VMEM((steps, seqs), jnp.float32),
             ),
             in_specs=[anywhere] * 4,
             out_specs=(vmem, vmem, vmem),
@@ -204,6 +213,13 @@
                 collective_id=0, has_side_effects=True, vmem_limit_bytes=60 * 1024 * 1024
             ),
         )(hidden.transpose(1, 0, 2), draft_ids.T, norm_gain.reshape(dim // LANES, LANES), head_w.T)
+        logp, log_norm, entropy = pl.pallas_call(
+            store_kernel,
+            out_shape=tuple(jax.ShapeDtypeStruct(r.shape, r.dtype) for r in results),
+            in_specs=[vmem] * len(results),
+            out_specs=(anywhere,) * len(results),
+            scratch_shapes=[pltpu.SemaphoreType.DMA((len(results),))],
+        )(*(pltpu.with_memory_space_constraint(r, pltpu.VMEM) for r in results))
         return logp.T, log_norm.T, entropy.T
 
     specs_in = (P('dp', None, None), P('dp', None), P(None), P(None, 'tp'))

time: 26.5 us -> 22.7 us (0.86)
  local copies, waits for them, and re-layouts: 3.71 us -> 0 us
    unnamed x3 -> x0, local copies, waits for them, and re-layouts: 3.71 us -> none
    pallas_call x1 -> x2, Pallas kernels: 22 us -> 22 us  [the longest x1 21.4 us: per_device(): pl.pallas_call(functools.partial(head_kernel, peers), out_shape=(pltpu.VM...]
where the time goes in v3:
time: 22.7 us; the launch traced here: 22.6 us
  Pallas kernels  22 us (97%)
  between operations  0.64 us (3%)
    pallas_call x1, Pallas kernels, per_device(): pl.pallas_call(functools.partial(head_kernel, peers), out_shape=(pltpu.VM...  21.4 us
    pallas_call x1, Pallas kernels, per_device(): pl.pallas_call(store_kernel, out_shape=tuple((jax.ShapeDtypeStruct(r.shap...  0.6 us

profile of v3, /device:TPU:21, one launch (start us, length us, event | category | flops | bytes accessed | tf_op | source)
XLA Modules:
  0.0 22.6 jit_solution(12054646867902171738)
XLA Ops:
  0.6 21.4 %shard_map.67 = (f32[2,32]{1,0:T(2,128)S(1)}, f32[3,32]{1,0:T(4,128)S(1)}, f32[3,32]{1,0:T(4,128)S(1)}) custom-call(bf16[3,32,4096]{2,1,0:T(8,128)(2,1)} %bitcast.8, s32[2,32]{1,0:T(2,128)} %bitcast.10, bf16[32,128]{1,0:T(8,128)(2,1)} %bitcast.9, bf16[2000,4096]{1,0:T(8,128)(2,1)} %bitcast.7), custom_call_target="tpu_custom_call" | custom-call | tf_op jit(solution)/shard_map/pallas_call | solution.py:188
  22.0 0.6 %shard_map.68 = (f32[2,32]{1,0:T(2,128)}, f32[3,32]{1,0:T(4,128)}, f32[3,32]{1,0:T(4,128)}) custom-call(f32[2,32]{1,0:T(2,128)S(1)} %get-tuple-element.9.refs_0_, f32[3,32]{1,0:T(4,128)S(1)} %get-tuple-element.10.refs_1_, f32[3,32]{1,0:T(4,128)S(1)} %get-tuple-element.11.refs_2_), custom_call_target="tpu_custom_call" | custom-call | tf_op jit(solution)/shard_map/pallas_call | solution.py:216

commit v4 on v0

v4 whole, which is shorter than its diff:
```python
import functools

import jax
import jax.numpy as jnp
from jax import lax
from jax.experimental import pallas as pl
from jax.experimental.pallas import tpu as pltpu
from jax.sharding import PartitionSpec as P

NORM_EPS = 1e-5
LANES = 128
SUBLANES = 8
PACKED = 16
CFG = {'sizes': (400,) * 5, 'window': 2}


def bounds_of(total, sizes):
    out, start = [], 0
    for size in sizes:
        size = min(size, total - start)
        if size:
            out.append((start, size))
        start += size
    out.extend((begin, min(sizes[-1], total - begin)) for begin in range(start, total, sizes[-1]))
    return out


def stats_of(carry, local_ids, start, tiles):
    top, exp_sum, weighted, picked = carry
    size, lanes = tiles.shape
    tiles = tiles.reshape(size // SUBLANES, SUBLANES, lanes)
    col_ids = lax.broadcasted_iota(jnp.int32, tiles.shape, 0) * SUBLANES + (
        lax.broadcasted_iota(jnp.int32, tiles.shape, 1) + start
    )
    hit = jnp.sum(jnp.where(col_ids == local_ids[None, :, :lanes], tiles, 0.0), axis=0)
    chunk_top = jnp.max(tiles, axis=0)
    new_top = chunk_top if top is None else jnp.maximum(top, chunk_top)
    shifted = tiles - new_top[None]
    exp_vals = jnp.exp(shifted)
    chunk_sum = jnp.sum(exp_vals, axis=0)
    chunk_weighted = jnp.sum(exp_vals * shifted, axis=0)
    if top is None:
        return new_top, chunk_sum, chunk_weighted, hit
    drop = top - new_top
    scale = jnp.exp(drop)
    return (
        new_top,
        chunk_sum + scale * exp_sum,
        chunk_weighted + scale * (weighted + exp_sum * drop),
        picked + hit,
    )


def fold(carry):
    top, exp_sum, weighted, picked = carry
    all_top = jnp.max(top, axis=0, keepdims=True)
    drop = top - all_top
    scale = jnp.exp(drop)
    rows = [
        all_top,
        jnp.sum(scale * exp_sum, axis=0, keepdims=True),
        jnp.sum(scale * (weighted + exp_sum * drop), axis=0, keepdims=True),
        jnp.sum(picked, axis=0, keepdims=True),
    ]
    stats = jnp.concatenate(rows, axis=0)
    lanes = stats.shape[1]
    if lanes < LANES:
        stats = jnp.concatenate([stats, jnp.zeros((stats.shape[0], LANES - lanes), jnp.float32)], axis=1)
    return stats


def local_scratch(steps, seqs, drafts, dim, cols, pieces):
    return [
        pltpu.VMEM((steps, seqs, dim), jnp.bfloat16),
        pltpu.VMEM((drafts, seqs), jnp.int32),
        pltpu.VMEM((dim // LANES, LANES), jnp.bfloat16),
        pltpu.VMEM((dim // LANES, LANES), jnp.float32),
        pltpu.VMEM((steps * seqs, dim), jnp.bfloat16),
        pltpu.VMEM((cols, dim), jnp.bfloat16),
        pltpu.SemaphoreType.DMA((steps,)),
        pltpu.SemaphoreType.DMA((2,)),
        pltpu.SemaphoreType.DMA((pieces,)),
    ]


def local_stats(cfg, me, x_hbm, ids_hbm, gain_hbm, w_hbm, x_vmem, ids_vmem, gain_vmem, gain_wide, n_vmem, w_vmem,
                x_sem, small_sem, w_sem, started=None):
    steps, seqs, dim = x_vmem.shape
    drafts = ids_vmem.shape[0]
    cols = w_vmem.shape[0]
    chunks = bounds_of(cols, cfg['sizes'])

    gain_copy = pltpu.make_async_copy(gain_hbm, gain_vmem, small_sem.at[1])
    ids_copy = pltpu.make_async_copy(ids_hbm, ids_vmem, small_sem.at[0])
    x_copies = [pltpu.make_async_copy(x_hbm.at[t], x_vmem.at[t], x_sem.at[t]) for t in range(steps)]
    w_copies = [
        pltpu.make_async_copy(w_hbm.at[pl.ds(start, size)], w_vmem.at[pl.ds(start, size)], w_sem.at[i])
        for i, (start, size) in enumerate(chunks)
    ]
    window = cfg['window']
    for copy in [gain_copy] + x_copies + [ids_copy] + w_copies[:window]:
        copy.start()
    if started is not None:
        started()

    def arrived(i):
        w_copies[i].wait()
        if i + window < len(chunks):
            w_copies[i + window].start()

    groups = [(t, g) for t in range(steps) for g in range(0, seqs, PACKED)]

    def block(t, g, c):
        return x_vmem[t, pl.ds(g, PACKED), pl.ds(c * LANES, LANES)].astype(jnp.float32)

    inv_rms = {}

    def squares(t, g):
        sums = [None] * 4
        for c in range(dim // LANES):
            x = block(t, g, c)
            sums[c % 4] = x * x if sums[c % 4] is None else sums[c % 4] + x * x
        mean = jnp.sum((sums[0] + sums[1]) + (sums[2] + sums[3]), axis=-1, keepdims=True) / dim
        inv_rms[t, g] = lax.rsqrt(mean + NORM_EPS)

    gain_copy.wait()
    gain_wide[...] = gain_vmem[...].astype(jnp.float32)
    for t in range(steps):
        x_copies[t].wait()
        for tt, g in groups:
            if tt == t:
                squares(t, g)
    ids_copy.wait()
    ids = jnp.concatenate(
        [ids_vmem[pl.ds(t, 1), :] for t in range(drafts)] + [jnp.full((1, LANES - drafts * seqs), -1, jnp.int32)],
        axis=1,
    )
    local_ids = ids - me * cols
    arrived(0)
    for c in range(dim // LANES):
        for t, g in groups:
            n = block(t, g, c) * inv_rms[t, g] * gain_wide[pl.ds(c, 1), :]
            n_vmem[pl.ds(t * seqs + g, PACKED), pl.ds(c * LANES, LANES)] = n.astype(jnp.bfloat16)

    carry = (None,) * 4
    pending = []
    for i, (start, size) in enumerate(chunks):
        if i:
            arrived(i)
        first = -(-size // 2 // PACKED) * PACKED
        outs = []
        for begin, part in ((start, first), (start + first, size - first)):
            outs.append((begin, lax.dot_general(
                w_vmem[pl.ds(begin, part), :], n_vmem[...], (((1,), (1,)), ((), ())),
                preferred_element_type=jnp.float32,
            )))
        for begin, tiles in pending:
            carry = stats_of(carry, local_ids, begin, tiles)
        pending = outs
    for begin, tiles in pending:
        carry = stats_of(carry, local_ids, begin, tiles)
    return fold(carry)


def head_kernel(
    cfg, peers,
    x_hbm, ids_hbm, gain_hbm, w_hbm,
    logp_ref, norm_ref, ent_ref,
    own, recv, send_sem, recv_sem, *scratch,
):
    steps, seqs, _ = scratch[0].shape
    drafts = scratch[1].shape[0]
    me = lax.axis_index('tp')
    hops = sorted(range(1, peers), key=lambda hop: -min(hop, peers - hop))
    targets = [lax.rem(me + hop, peers) for hop in hops]
    barrier = pltpu.get_barrier_semaphore()

    def announce():
        for target in targets:
            pl.semaphore_signal(barrier, inc=1, device_id={'tp': target}, device_id_type=pl.DeviceIdType.MESH)

    stats = local_stats(cfg, me, x_hbm, ids_hbm, gain_hbm, w_hbm, *scratch, started=announce)
    own[...] = stats
    recv[:, pl.ds(me, 1), :] = stats[:, None, :]

    pl.semaphore_wait(barrier, peers - 1)
    for target in targets:
        pltpu.make_async_remote_copy(
            src_ref=own, dst_ref=recv.at[:, me], send_sem=send_sem, recv_sem=recv_sem,
            device_id={'tp': target}, device_id_type=pl.DeviceIdType.MESH,
        ).start()
    others = recv.at[:, pl.ds(0, peers - 1)]
    pltpu.make_async_copy(others, others, recv_sem).wait()

    tops, sums, weights, picks = (recv[i] for i in range(4))
    full_top = jnp.max(tops, axis=0, keepdims=True)
    drop = tops - full_top
    scale = jnp.exp(drop)
    full_sum = jnp.sum(scale * sums, axis=0, keepdims=True)
    full_weighted = jnp.sum(scale * (weights + sums * drop), axis=0, keepdims=True)
    full_picked = jnp.sum(picks, axis=0, keepdims=True)
    log_sum = jnp.log(full_sum)
    log_norm = full_top + log_sum
    entropy = log_sum - full_weighted / full_sum
    logp = full_picked - log_norm
    for t in range(steps):
        lanes = slice(t * seqs, (t + 1) * seqs)
        norm_ref[pl.ds(t, 1), :] = log_norm[:, lanes]
        ent_ref[pl.ds(t, 1), :] = entropy[:, lanes]
        if t < drafts:
            logp_ref[pl.ds(t, 1), :] = logp[:, lanes]
    pltpu.make_async_copy(others, others, send_sem).wait()


def store_kernel(*refs):
    count = (len(refs) - 1) // 2
    copies = [pltpu.make_async_copy(refs[i], refs[count + i], refs[-1].at[i]) for i in range(count)]
    for copy in copies:
        copy.start()
    for copy in copies:
        copy.wait()


def solution(mesh):
    peers = mesh.shape['tp']

    def per_device(hidden, draft_ids, norm_gain, head_w):
        seqs, steps, dim = hidden.shape
        drafts = draft_ids.shape[1]
        cols = head_w.shape[1]
        vmem = pl.BlockSpec(memory_space=pltpu.VMEM)
        results = pl.pallas_call(
            functools.partial(head_kernel, CFG, peers),
            out_shape=tuple(pltpu.VMEM((n, seqs), jnp.float32) for n in (drafts, steps, steps)),
            in_specs=[pl.BlockSpec(memory_space=pltpu.HBM)] * 4,
            out_specs=(vmem,) * 3,
            scratch_shapes=[
                pltpu.VMEM((4, LANES), jnp.float32),
                pltpu.VMEM((4, peers, LANES), jnp.float32),
                pltpu.SemaphoreType.DMA,
                pltpu.SemaphoreType.DMA,
            ] + local_scratch(steps, seqs, drafts, dim, cols, len(bounds_of(cols, CFG['sizes']))),
            compiler_params=pltpu.CompilerParams(
                collective_id=0, has_side_effects=True, vmem_limit_bytes=60 * 1024 * 1024
            ),
        )(
            *(
                pltpu.with_memory_space_constraint(a, pltpu.HBM)
                for a in (hidden.transpose(1, 0, 2), draft_ids.T, norm_gain.reshape(dim // LANES, LANES), head_w.T)
            )
        )
        logp, log_norm, entropy = pl.pallas_call(
            store_kernel,
            out_shape=tuple(jax.ShapeDtypeStruct(r.shape, r.dtype) for r in results),
            in_specs=[vmem] * len(results),
            out_specs=(pl.BlockSpec(memory_space=pl.ANY),) * len(results),
            scratch_shapes=[pltpu.SemaphoreType.DMA((len(results),))],
        )(*(pltpu.with_memory_space_constraint(r, pltpu.VMEM) for r in results))
        return logp.T, log_norm.T, entropy.T

    specs_in = (P('dp', None, None), P('dp', None), P(None), P(None, 'tp'))
    specs_out = (P('dp', None), P('dp', None), P('dp', None))
    return jax.shard_map(per_device, mesh=mesh, in_specs=specs_in, out_specs=specs_out, check_vma=False)
```

time: 123 us -> 20 us (0.16)
  waiting for transfers between devices: 77.4 us -> 0 us
  other arithmetic: 19.3 us -> 0 us
  Pallas kernels: 0 us -> 19.2 us
  between operations: 14.1 us -> 0.64 us
  matrix products: 12 us -> 0 us
    all_gather x1 -> x0, waiting for transfers between devices: 77.3 us -> none  [per_device(): gathered = lax.all_gather(logits, 'tp')]
    pallas_call x0 -> x2, Pallas kernels: none -> 19.2 us  [the longest x1 18.6 us: per_device(): pl.pallas_call(functools.partial(head_kernel, CFG, peers), out_shape=tupl...]
    reduce_sum x3 -> x0, other arithmetic: 12.1 us -> none  [the longest x1 8.68 us: per_device(): weighted = jnp.sum(exp_vals * shifted, axis=(0, 3))]
    dot_general x1 -> x0, matrix products: 12 us -> none  [per_device(): jnp.einsum('btd,dv->btv', normed, head_w, preferred_element_type=jnp.floa...]
    reduce_max x2 -> x0, other arithmetic: 5.23 us -> none  [per_device(): row_max = jnp.max(gathered, axis=(0, 3))]
  transfers between devices with their start and end apart: 1 -> 0, of which waited for: 1 -> 0; matrix products, arithmetic and copies ran while one was open for 0% -> 0% of each run, Pallas kernels for 0% -> 0%
where the time goes in v4:
time: 20 us; the launch traced here: 19.9 us
  Pallas kernels  19.2 us (96%)
  between operations  0.64 us (3%)
    pallas_call x1, Pallas kernels, per_device(): pl.pallas_call(functools.partial(head_kernel, CFG, peers), out_shape=tupl...  18.6 us
    pallas_call x1, Pallas kernels, per_device(): pl.pallas_call(store_kernel, out_shape=tuple((jax.ShapeDtypeStruct(r.shap...  0.6 us

profile of v4, /device:TPU:21, one launch (start us, length us, event | category | flops | bytes accessed | tf_op | source)
XLA Modules:
  0.0 19.9 jit_solution(16537203153660342054)
XLA Ops:
  0.6 18.6 %shard_map.67 = (f32[2,32]{1,0:T(2,128)S(1)}, f32[3,32]{1,0:T(4,128)S(1)}, f32[3,32]{1,0:T(4,128)S(1)}) custom-call(bf16[3,32,4096]{2,1,0:T(8,128)(2,1)} %bitcast.8, s32[2,32]{1,0:T(2,128)} %bitcast.10, bf16[32,128]{1,0:T(8,128)(2,1)} %bitcast.9, bf16[2000,4096]{1,0:T(8,128)(2,1)} %bitcast.7), custom_call_target="tpu_custom_call" | custom-call | tf_op jit(solution)/shard_map/pallas_call | solution.py:232
  19.3 0.6 %shard_map.68 = (f32[2,32]{1,0:T(2,128)}, f32[3,32]{1,0:T(4,128)}, f32[3,32]{1,0:T(4,128)}) custom-call(f32[2,32]{1,0:T(2,128)S(1)} %get-tuple-element.9.refs_0_, f32[3,32]{1,0:T(4,128)S(1)} %get-tuple-element.10.refs_1_, f32[3,32]{1,0:T(4,128)S(1)} %get-tuple-element.11.refs_2_), custom_call_target="tpu_custom_call" | custom-call | tf_op jit(solution)/shard_map/pallas_call | solution.py:252

commit v5 on v4

--- a/solution.py
+++ b/solution.py
@@ -11,17 +11,18 @@
 LANES = 128
 SUBLANES = 8
 PACKED = 16
-CFG = {'sizes': (400,) * 5, 'window': 2}
-
-
-def bounds_of(total, sizes):
+CFG = {'plan': ((800, (1, 1, 1, 1)), (800, (1, 1, 1, 1)), (400, (1, 1, 1, 1))), 'window': 3}
+
+
+def pieces_of(total, dim, plan):
     out, start = [], 0
-    for size in sizes:
-        size = min(size, total - start)
-        if size:
-            out.append((start, size))
-        start += size
-    out.extend((begin, min(sizes[-1], total - begin)) for begin in range(start, total, sizes[-1]))
+    for rows, cuts in plan:
+        rows = min(rows, total - start)
+        edges = [dim * cut // sum(cuts) for cut in (sum(cuts[:j]) for j in range(len(cuts) + 1))]
+        for low, high in zip(edges, edges[1:]):
+            out.append((start, rows, low, high - low, high == dim))
+        start += rows
+    assert start == total
     return out
 
 
@@ -88,15 +89,15 @@
     steps, seqs, dim = x_vmem.shape
     drafts = ids_vmem.shape[0]
     cols = w_vmem.shape[0]
-    chunks = bounds_of(cols, cfg['sizes'])
+    chunks = pieces_of(cols, dim, cfg['plan'])
 
     gain_copy = pltpu.make_async_copy(gain_hbm, gain_vmem, small_sem.at[1])
     ids_copy = pltpu.make_async_copy(ids_hbm, ids_vmem, small_sem.at[0])
     x_copies = [pltpu.make_async_copy(x_hbm.at[t], x_vmem.at[t], x_sem.at[t]) for t in range(steps)]
-    w_copies = [
-        pltpu.make_async_copy(w_hbm.at[pl.ds(start, size)], w_vmem.at[pl.ds(start, size)], w_sem.at[i])
-        for i, (start, size) in enumerate(chunks)
-    ]
+    w_copies = []
+    for i, (start, size, low, depth, _) in enumerate(chunks):
+        where = (pl.ds(start, size), pl.ds(low, depth))
+        w_copies.append(pltpu.make_async_copy(w_hbm.at[where], w_vmem.at[where], w_sem.at[i]))
     window = cfg['window']
     for copy in [gain_copy] + x_copies + [ids_copy] + w_copies[:window]:
         copy.start()
@@ -136,27 +137,37 @@
         axis=1,
     )
     local_ids = ids - me * cols
-    arrived(0)
-    for c in range(dim // LANES):
-        for t, g in groups:
-            n = block(t, g, c) * inv_rms[t, g] * gain_wide[pl.ds(c, 1), :]
-            n_vmem[pl.ds(t * seqs + g, PACKED), pl.ds(c * LANES, LANES)] = n.astype(jnp.bfloat16)
-
+    done = [0]
+
+    def normalise(low, high):
+        for c in range(max(low, done[0]) // LANES, high // LANES):
+            for t, g in groups:
+                n = block(t, g, c) * inv_rms[t, g] * gain_wide[pl.ds(c, 1), :]
+                n_vmem[pl.ds(t * seqs + g, PACKED), pl.ds(c * LANES, LANES)] = n.astype(jnp.bfloat16)
+        done[0] = max(done[0], high)
+
+    normalise(0, chunks[0][3])
     carry = (None,) * 4
     pending = []
-    for i, (start, size) in enumerate(chunks):
-        if i:
-            arrived(i)
+    outs = None
+    for i, (start, size, low, depth, last) in enumerate(chunks):
+        arrived(i)
         first = -(-size // 2 // PACKED) * PACKED
-        outs = []
-        for begin, part in ((start, first), (start + first, size - first)):
-            outs.append((begin, lax.dot_general(
-                w_vmem[pl.ds(begin, part), :], n_vmem[...], (((1,), (1,)), ((), ())),
+        terms = [
+            (begin, lax.dot_general(
+                w_vmem[pl.ds(begin, part), pl.ds(low, depth)], n_vmem[:, pl.ds(low, depth)], (((1,), (1,)), ((), ())),
                 preferred_element_type=jnp.float32,
-            )))
+            ))
+            for begin, part in ((start, first), (start + first, size - first))
+        ]
+        if i + 1 < len(chunks) and low + depth < dim:
+            normalise(chunks[i + 1][2], chunks[i + 1][2] + chunks[i + 1][3])
+        outs = terms if outs is None else [(begin, a + b) for (begin, a), (_, b) in zip(outs, terms)]
         for begin, tiles in pending:
             carry = stats_of(carry, local_ids, begin, tiles)
-        pending = outs
+        pending = []
+        if last:
+            pending, outs = outs, None
     for begin, tiles in pending:
         carry = stats_of(carry, local_ids, begin, tiles)
     return fold(carry)
@@ -239,7 +250,7 @@
                 pltpu.VMEM((4, peers, LANES), jnp.float32),
                 pltpu.SemaphoreType.DMA,
                 pltpu.SemaphoreType.DMA,
-            ] + local_scratch(steps, seqs, drafts, dim, cols, len(bounds_of(cols, CFG['sizes']))),
+            ] + local_scratch(steps, seqs, drafts, dim, cols, len(pieces_of(cols, dim, CFG['plan']))),
             compiler_params=pltpu.CompilerParams(
                 collective_id=0, has_side_effects=True, vmem_limit_bytes=60 * 1024 * 1024
             ),

time: 20 us -> 21.1 us (1.055)
  Pallas kernels: 19.2 us -> 20.3 us
    pallas_call x1, Pallas kernels: 18.6 us -> 19.7 us  [per_device(): pl.pallas_call(functools.partial(head_kernel, CFG, peers), out_shape=tupl...]
where the time goes in v5:
time: 21.1 us; the launch traced here: 20.9 us
  Pallas kernels  20.3 us (96%)
  between operations  0.64 us (3%)
    pallas_call x1, Pallas kernels, per_device(): pl.pallas_call(functools.partial(head_kernel, CFG, peers), out_shape=tupl...  19.7 us
    pallas_call x1, Pallas kernels, per_device(): pl.pallas_call(store_kernel, out_shape=tuple((jax.ShapeDtypeStruct(r.shap...  0.6 us

profile of v5, /device:TPU:21, one launch (start us, length us, event | category | flops | bytes accessed | tf_op | source)
XLA Modules:
  0.0 20.9 jit_solution(1609686162715136071)
XLA Ops:
  0.6 19.7 %shard_map.67 = (f32[2,32]{1,0:T(2,128)S(1)}, f32[3,32]{1,0:T(4,128)S(1)}, f32[3,32]{1,0:T(4,128)S(1)}) custom-call(bf16[3,32,4096]{2,1,0:T(8,128)(2,1)} %bitcast.8, s32[2,32]{1,0:T(2,128)} %bitcast.10, bf16[32,128]{1,0:T(8,128)(2,1)} %bitcast.9, bf16[2000,4096]{1,0:T(8,128)(2,1)} %bitcast.7), custom_call_target="tpu_custom_call" | custom-call | tf_op jit(solution)/shard_map/pallas_call | solution.py:243
  20.3 0.6 %shard_map.68 = (f32[2,32]{1,0:T(2,128)}, f32[3,32]{1,0:T(4,128)}, f32[3,32]{1,0:T(4,128)}) custom-call(f32[2,32]{1,0:T(2,128)S(1)} %get-tuple-element.9.refs_0_, f32[3,32]{1,0:T(4,128)S(1)} %get-tuple-element.10.refs_1_, f32[3,32]{1,0:T(4,128)S(1)} %get-tuple-element.11.refs_2_), custom_call_target="tpu_custom_call" | custom-call | tf_op jit(solution)/shard_map/pallas_call | solution.py:263

commit v6 on v4

--- a/solution.py
+++ b/solution.py
@@ -11,7 +11,7 @@
 LANES = 128
 SUBLANES = 8
 PACKED = 16
-CFG = {'sizes': (400,) * 5, 'window': 2}
+CFG = {'sizes': (400,) * 5}
 
 
 def bounds_of(total, sizes):
@@ -84,7 +84,7 @@
 
 
 def local_stats(cfg, me, x_hbm, ids_hbm, gain_hbm, w_hbm, x_vmem, ids_vmem, gain_vmem, gain_wide, n_vmem, w_vmem,
-                x_sem, small_sem, w_sem, started=None):
+                x_sem, small_sem, w_sem, announce):
     steps, seqs, dim = x_vmem.shape
     drafts = ids_vmem.shape[0]
     cols = w_vmem.shape[0]
@@ -97,16 +97,12 @@
         pltpu.make_async_copy(w_hbm.at[pl.ds(start, size)], w_vmem.at[pl.ds(start, size)], w_sem.at[i])
         for i, (start, size) in enumerate(chunks)
     ]
-    window = cfg['window']
-    for copy in [gain_copy] + x_copies + [ids_copy] + w_copies[:window]:
+    for copy in [gain_copy] + x_copies + [ids_copy]:
         copy.start()
-    if started is not None:
-        started()
-
-    def arrived(i):
-        w_copies[i].wait()
-        if i + window < len(chunks):
-            w_copies[i + window].start()
+    announce(0, 1)
+    for copy in w_copies:
+        copy.start()
+    announce(1, None)
 
     groups = [(t, g) for t in range(steps) for g in range(0, seqs, PACKED)]
 
@@ -136,7 +132,7 @@
         axis=1,
     )
     local_ids = ids - me * cols
-    arrived(0)
+    w_copies[0].wait()
     for c in range(dim // LANES):
         for t, g in groups:
             n = block(t, g, c) * inv_rms[t, g] * gain_wide[pl.ds(c, 1), :]
@@ -146,7 +142,7 @@
     pending = []
     for i, (start, size) in enumerate(chunks):
         if i:
-            arrived(i)
+            w_copies[i].wait()
         first = -(-size // 2 // PACKED) * PACKED
         outs = []
         for begin, part in ((start, first), (start + first, size - first)):
@@ -175,11 +171,11 @@
     targets = [lax.rem(me + hop, peers) for hop in hops]
     barrier = pltpu.get_barrier_semaphore()
 
-    def announce():
-        for target in targets:
+    def announce(begin, end):
+        for target in targets[begin:end]:
             pl.semaphore_signal(barrier, inc=1, device_id={'tp': target}, device_id_type=pl.DeviceIdType.MESH)
 
-    stats = local_stats(cfg, me, x_hbm, ids_hbm, gain_hbm, w_hbm, *scratch, started=announce)
+    stats = local_stats(cfg, me, x_hbm, ids_hbm, gain_hbm, w_hbm, *scratch, announce)
     own[...] = stats
     recv[:, pl.ds(me, 1), :] = stats[:, None, :]
 

time: 20 us -> 19.7 us (0.985)
    pallas_call x1, Pallas kernels: 18.6 us -> 18.4 us  [per_device(): pl.pallas_call(functools.partial(head_kernel, CFG, peers), out_shape=tupl...]
where the time goes in v6:
time: 19.7 us; the launch traced here: 19.6 us
  Pallas kernels  19 us (96%)
  between operations  0.64 us (3%)
    pallas_call x1, Pallas kernels, per_device(): pl.pallas_call(functools.partial(head_kernel, CFG, peers), out_shape=tupl...  18.4 us
    pallas_call x1, Pallas kernels, per_device(): pl.pallas_call(store_kernel, out_shape=tuple((jax.ShapeDtypeStruct(r.shap...  0.6 us

profile of v6, /device:TPU:21, one launch (start us, length us, event | category | flops | bytes accessed | tf_op | source)
XLA Modules:
  0.0 19.6 jit_solution(17262557758892791702)
XLA Ops:
  0.6 18.4 %shard_map.67 = (f32[2,32]{1,0:T(2,128)S(1)}, f32[3,32]{1,0:T(4,128)S(1)}, f32[3,32]{1,0:T(4,128)S(1)}) custom-call(bf16[3,32,4096]{2,1,0:T(8,128)(2,1)} %bitcast.8, s32[2,32]{1,0:T(2,128)} %bitcast.10, bf16[32,128]{1,0:T(8,128)(2,1)} %bitcast.9, bf16[2000,4096]{1,0:T(8,128)(2,1)} %bitcast.7), custom_call_target="tpu_custom_call" | custom-call | tf_op jit(solution)/shard_map/pallas_call | solution.py:228
  19.0 0.6 %shard_map.68 = (f32[2,32]{1,0:T(2,128)}, f32[3,32]{1,0:T(4,128)}, f32[3,32]{1,0:T(4,128)}) custom-call(f32[2,32]{1,0:T(2,128)S(1)} %get-tuple-element.9.refs_0_, f32[3,32]{1,0:T(4,128)S(1)} %get-tuple-element.10.refs_1_, f32[3,32]{1,0:T(4,128)S(1)} %get-tuple-element.11.refs_2_), custom_call_target="tpu_custom_call" | custom-call | tf_op jit(solution)/shard_map/pallas_call | solution.py:248

commit v7 on v6

--- a/solution.py
+++ b/solution.py
@@ -11,7 +11,7 @@
 LANES = 128
 SUBLANES = 8
 PACKED = 16
-CFG = {'sizes': (400,) * 5}
+CFG = {'sizes': (224, 256, 320, 384, 432, 384)}
 
 
 def bounds_of(total, sizes):
@@ -51,22 +51,22 @@
     )
 
 
-def fold(carry):
+def fold(carry, rows, drafts):
     top, exp_sum, weighted, picked = carry
     all_top = jnp.max(top, axis=0, keepdims=True)
     drop = top - all_top
     scale = jnp.exp(drop)
-    rows = [
+    out = [
         all_top,
         jnp.sum(scale * exp_sum, axis=0, keepdims=True),
         jnp.sum(scale * (weighted + exp_sum * drop), axis=0, keepdims=True),
-        jnp.sum(picked, axis=0, keepdims=True),
     ]
-    stats = jnp.concatenate(rows, axis=0)
-    lanes = stats.shape[1]
-    if lanes < LANES:
-        stats = jnp.concatenate([stats, jnp.zeros((stats.shape[0], LANES - lanes), jnp.float32)], axis=1)
-    return stats
+    picked = jnp.sum(picked, axis=0, keepdims=True)
+    spare = LANES - rows
+    for t in range(len(out)):
+        lanes = picked[:, t * spare:(t + 1) * spare] if t < drafts else jnp.zeros((1, spare), jnp.float32)
+        out[t] = jnp.concatenate([out[t], lanes], axis=1)
+    return jnp.concatenate(out, axis=0)
 
 
 def local_scratch(steps, seqs, drafts, dim, cols, pieces):
@@ -155,7 +155,7 @@
         pending = outs
     for begin, tiles in pending:
         carry = stats_of(carry, local_ids, begin, tiles)
-    return fold(carry)
+    return fold(carry, steps * seqs, drafts)
 
 
 def head_kernel(
@@ -167,8 +167,7 @@
     steps, seqs, _ = scratch[0].shape
     drafts = scratch[1].shape[0]
     me = lax.axis_index('tp')
-    hops = sorted(range(1, peers), key=lambda hop: -min(hop, peers - hop))
-    targets = [lax.rem(me + hop, peers) for hop in hops]
+    targets = [other + jnp.where(other >= me, 1, 0) for other in range(peers - 1)]
     barrier = pltpu.get_barrier_semaphore()
 
     def announce(begin, end):
@@ -188,23 +187,22 @@
     others = recv.at[:, pl.ds(0, peers - 1)]
     pltpu.make_async_copy(others, others, recv_sem).wait()
 
-    tops, sums, weights, picks = (recv[i] for i in range(4))
+    tops, sums, weights = (recv[i] for i in range(3))
     full_top = jnp.max(tops, axis=0, keepdims=True)
     drop = tops - full_top
     scale = jnp.exp(drop)
     full_sum = jnp.sum(scale * sums, axis=0, keepdims=True)
     full_weighted = jnp.sum(scale * (weights + sums * drop), axis=0, keepdims=True)
-    full_picked = jnp.sum(picks, axis=0, keepdims=True)
     log_sum = jnp.log(full_sum)
     log_norm = full_top + log_sum
     entropy = log_sum - full_weighted / full_sum
-    logp = full_picked - log_norm
     for t in range(steps):
         lanes = slice(t * seqs, (t + 1) * seqs)
         norm_ref[pl.ds(t, 1), :] = log_norm[:, lanes]
         ent_ref[pl.ds(t, 1), :] = entropy[:, lanes]
         if t < drafts:
-            logp_ref[pl.ds(t, 1), :] = logp[:, lanes]
+            picked = jnp.sum(recv[t], axis=0, keepdims=True)[:, steps * seqs:]
+            logp_ref[pl.ds(t, 1), :] = picked - log_norm[:, lanes]
     pltpu.make_async_copy(others, others, send_sem).wait()
 
 
@@ -224,6 +222,7 @@
         seqs, steps, dim = hidden.shape
         drafts = draft_ids.shape[1]
         cols = head_w.shape[1]
+        assert steps >= drafts and seqs == LANES - steps * seqs
         vmem = pl.BlockSpec(memory_space=pltpu.VMEM)
         results = pl.pallas_call(
             functools.partial(head_kernel, CFG, peers),
@@ -231,8 +230,8 @@
             in_specs=[pl.BlockSpec(memory_space=pltpu.HBM)] * 4,
             out_specs=(vmem,) * 3,
             scratch_shapes=[
-                pltpu.VMEM((4, LANES), jnp.float32),
-                pltpu.VMEM((4, peers, LANES), jnp.float32),
+                pltpu.VMEM((3, LANES), jnp.float32),
+                pltpu.VMEM((3, peers, LANES), jnp.float32),
                 pltpu.SemaphoreType.DMA,
                 pltpu.SemaphoreType.DMA,
             ] + local_scratch(steps, seqs, drafts, dim, cols, len(bounds_of(cols, CFG['sizes']))),

time: 19.7 us -> 19.6 us (level)
  no operation moved by 1% of the time
where the time goes in v7:
time: 19.6 us; the launch traced here: 19.5 us
  Pallas kernels  18.9 us (96%)
  between operations  0.64 us (3%)
    pallas_call x1, Pallas kernels, per_device(): pl.pallas_call(functools.partial(head_kernel, CFG, peers), out_shape=tupl...  18.3 us
    pallas_call x1, Pallas kernels, per_device(): pl.pallas_call(store_kernel, out_shape=tuple((jax.ShapeDtypeStruct(r.shap...  0.6 us

profile of v7, /device:TPU:21, one launch (start us, length us, event | category | flops | bytes accessed | tf_op | source)
XLA Modules:
  0.0 19.5 jit_solution(9197059169329345292)
XLA Ops:
  0.6 18.3 %shard_map.67 = (f32[2,32]{1,0:T(2,128)S(1)}, f32[3,32]{1,0:T(4,128)S(1)}, f32[3,32]{1,0:T(4,128)S(1)}) custom-call(bf16[3,32,4096]{2,1,0:T(8,128)(2,1)} %bitcast.8, s32[2,32]{1,0:T(2,128)} %bitcast.10, bf16[32,128]{1,0:T(8,128)(2,1)} %bitcast.9, bf16[2000,4096]{1,0:T(8,128)(2,1)} %bitcast.7), custom_call_target="tpu_custom_call" | custom-call | tf_op jit(solution)/shard_map/pallas_call | solution.py:227
  18.9 0.6 %shard_map.68 = (f32[2,32]{1,0:T(2,128)}, f32[3,32]{1,0:T(4,128)}, f32[3,32]{1,0:T(4,128)}) custom-call(f32[2,32]{1,0:T(2,128)S(1)} %get-tuple-element.9.refs_0_, f32[3,32]{1,0:T(4,128)S(1)} %get-tuple-element.10.refs_1_, f32[3,32]{1,0:T(4,128)S(1)} %get-tuple-element.11.refs_2_), custom_call_target="tpu_custom_call" | custom-call | tf_op jit(solution)/shard_map/pallas_call | solution.py:247

commit v8 on v7

--- a/solution.py
+++ b/solution.py
@@ -11,7 +11,7 @@
 LANES = 128
 SUBLANES = 8
 PACKED = 16
-CFG = {'sizes': (224, 256, 320, 384, 432, 384)}
+CFG = {'sizes': (208, 256, 304, 368, 400, 464)}
 
 
 def bounds_of(total, sizes):
@@ -97,7 +97,7 @@
         pltpu.make_async_copy(w_hbm.at[pl.ds(start, size)], w_vmem.at[pl.ds(start, size)], w_sem.at[i])
         for i, (start, size) in enumerate(chunks)
     ]
-    for copy in [gain_copy] + x_copies + [ids_copy]:
+    for copy in [gain_copy, ids_copy] + x_copies:
         copy.start()
     announce(0, 1)
     for copy in w_copies:
@@ -109,40 +109,36 @@
     def block(t, g, c):
         return x_vmem[t, pl.ds(g, PACKED), pl.ds(c * LANES, LANES)].astype(jnp.float32)
 
-    inv_rms = {}
-
-    def squares(t, g):
-        sums = [None] * 4
-        for c in range(dim // LANES):
-            x = block(t, g, c)
-            sums[c % 4] = x * x if sums[c % 4] is None else sums[c % 4] + x * x
-        mean = jnp.sum((sums[0] + sums[1]) + (sums[2] + sums[3]), axis=-1, keepdims=True) / dim
-        inv_rms[t, g] = lax.rsqrt(mean + NORM_EPS)
-
-    gain_copy.wait()
-    gain_wide[...] = gain_vmem[...].astype(jnp.float32)
-    for t in range(steps):
-        x_copies[t].wait()
-        for tt, g in groups:
-            if tt == t:
-                squares(t, g)
     ids_copy.wait()
     ids = jnp.concatenate(
         [ids_vmem[pl.ds(t, 1), :] for t in range(drafts)] + [jnp.full((1, LANES - drafts * seqs), -1, jnp.int32)],
         axis=1,
     )
     local_ids = ids - me * cols
-    w_copies[0].wait()
-    for c in range(dim // LANES):
-        for t, g in groups:
+    gain_copy.wait()
+    gain_wide[...] = gain_vmem[...].astype(jnp.float32)
+    squares = {}
+    for t in range(steps):
+        x_copies[t].wait()
+        for tt, g in groups:
+            if tt == t:
+                sums = [None] * 4
+                for c in range(dim // LANES):
+                    x = block(t, g, c)
+                    sums[c % 4] = x * x if sums[c % 4] is None else sums[c % 4] + x * x
+                squares[t, g] = (sums[0] + sums[1]) + (sums[2] + sums[3])
+    inv_rms = {}
+    for key in groups:
+        inv_rms[key] = lax.rsqrt(jnp.sum(squares[key], axis=-1, keepdims=True) / dim + NORM_EPS)
+    for t, g in groups:
+        for c in range(dim // LANES):
             n = block(t, g, c) * inv_rms[t, g] * gain_wide[pl.ds(c, 1), :]
             n_vmem[pl.ds(t * seqs + g, PACKED), pl.ds(c * LANES, LANES)] = n.astype(jnp.bfloat16)
 
     carry = (None,) * 4
     pending = []
     for i, (start, size) in enumerate(chunks):
-        if i:
-            w_copies[i].wait()
+        w_copies[i].wait()
         first = -(-size // 2 // PACKED) * PACKED
         outs = []
         for begin, part in ((start, first), (start + first, size - first)):

time: 19.6 us -> 19.6 us (level)
  no operation moved by 1% of the time
where the time goes in v8:
time: 19.6 us; the launch traced here: 19.5 us
  Pallas kernels  18.9 us (96%)
  between operations  0.64 us (3%)
    pallas_call x1, Pallas kernels, per_device(): pl.pallas_call(functools.partial(head_kernel, CFG, peers), out_shape=tupl...  18.3 us
    pallas_call x1, Pallas kernels, per_device(): pl.pallas_call(store_kernel, out_shape=tuple((jax.ShapeDtypeStruct(r.shap...  0.6 us

profile of v8, /device:TPU:21, one launch (start us, length us, event | category | flops | bytes accessed | tf_op | source)
XLA Modules:
  0.0 19.5 jit_solution(12336644059289689)
XLA Ops:
  0.6 18.3 %shard_map.67 = (f32[2,32]{1,0:T(2,128)S(1)}, f32[3,32]{1,0:T(4,128)S(1)}, f32[3,32]{1,0:T(4,128)S(1)}) custom-call(bf16[3,32,4096]{2,1,0:T(8,128)(2,1)} %bitcast.8, s32[2,32]{1,0:T(2,128)} %bitcast.10, bf16[32,128]{1,0:T(8,128)(2,1)} %bitcast.9, bf16[2000,4096]{1,0:T(8,128)(2,1)} %bitcast.7), custom_call_target="tpu_custom_call" | custom-call | tf_op jit(solution)/shard_map/pallas_call | solution.py:223
  18.9 0.6 %shard_map.68 = (f32[2,32]{1,0:T(2,128)}, f32[3,32]{1,0:T(4,128)}, f32[3,32]{1,0:T(4,128)}) custom-call(f32[2,32]{1,0:T(2,128)S(1)} %get-tuple-element.9.refs_0_, f32[3,32]{1,0:T(4,128)S(1)} %get-tuple-element.10.refs_1_, f32[3,32]{1,0:T(4,128)S(1)} %get-tuple-element.11.refs_2_), custom_call_target="tpu_custom_call" | custom-call | tf_op jit(solution)/shard_map/pallas_call | solution.py:243

commit v9 on v8

--- a/solution.py
+++ b/solution.py
@@ -11,7 +11,7 @@
 LANES = 128
 SUBLANES = 8
 PACKED = 16
-CFG = {'sizes': (208, 256, 304, 368, 400, 464)}
+CFG = {'sizes': (240, 320, 400, 416, 368, 256)}
 
 
 def bounds_of(total, sizes):
@@ -93,10 +93,12 @@
     gain_copy = pltpu.make_async_copy(gain_hbm, gain_vmem, small_sem.at[1])
     ids_copy = pltpu.make_async_copy(ids_hbm, ids_vmem, small_sem.at[0])
     x_copies = [pltpu.make_async_copy(x_hbm.at[t], x_vmem.at[t], x_sem.at[t]) for t in range(steps)]
-    w_copies = [
-        pltpu.make_async_copy(w_hbm.at[pl.ds(start, size)], w_vmem.at[pl.ds(start, size)], w_sem.at[i])
-        for i, (start, size) in enumerate(chunks)
-    ]
+    depths = (pl.ds(0, dim // 2), pl.ds(dim // 2, dim // 2))
+    w_copies = []
+    for i, (start, size) in enumerate(chunks):
+        for depth in depths:
+            where = (pl.ds(start, size), depth)
+            w_copies.append(pltpu.make_async_copy(w_hbm.at[where], w_vmem.at[where], w_sem.at[len(w_copies)]))
     for copy in [gain_copy, ids_copy] + x_copies:
         copy.start()
     announce(0, 1)
@@ -135,22 +137,29 @@
             n = block(t, g, c) * inv_rms[t, g] * gain_wide[pl.ds(c, 1), :]
             n_vmem[pl.ds(t * seqs + g, PACKED), pl.ds(c * LANES, LANES)] = n.astype(jnp.bfloat16)
 
+    def product(begin, part, depth):
+        return lax.dot_general(
+            w_vmem[pl.ds(begin, part), depth], n_vmem[:, depth], (((1,), (1,)), ((), ())),
+            preferred_element_type=jnp.float32,
+        )
+
     carry = (None,) * 4
-    pending = []
-    for i, (start, size) in enumerate(chunks):
-        w_copies[i].wait()
-        first = -(-size // 2 // PACKED) * PACKED
-        outs = []
-        for begin, part in ((start, first), (start + first, size - first)):
-            outs.append((begin, lax.dot_general(
-                w_vmem[pl.ds(begin, part), :], n_vmem[...], (((1,), (1,)), ((), ())),
-                preferred_element_type=jnp.float32,
-            )))
-        for begin, tiles in pending:
+    opened = []
+    for i in range(len(chunks) + 1):
+        if i:
+            w_copies[2 * i - 1].wait()
+        if i < len(chunks):
+            w_copies[2 * i].wait()
+        closed = [(begin, part, tiles + product(begin, part, depths[1])) for begin, part, tiles in opened]
+        opened = []
+        if i < len(chunks):
+            start, size = chunks[i]
+            first = -(-size // 2 // PACKED) * PACKED
+            for begin, part in ((start, first), (start + first, size - first)):
+                low, high = (product(begin, part, pl.ds(j * (dim // 4), dim // 4)) for j in range(2))
+                opened.append((begin, part, low + high))
+        for begin, _, tiles in closed:
             carry = stats_of(carry, local_ids, begin, tiles)
-        pending = outs
-    for begin, tiles in pending:
-        carry = stats_of(carry, local_ids, begin, tiles)
     return fold(carry, steps * seqs, drafts)
 
 
@@ -230,7 +239,7 @@
                 pltpu.VMEM((3, peers, LANES), jnp.float32),
                 pltpu.SemaphoreType.DMA,
                 pltpu.SemaphoreType.DMA,
-            ] + local_scratch(steps, seqs, drafts, dim, cols, len(bounds_of(cols, CFG['sizes']))),
+            ] + local_scratch(steps, seqs, drafts, dim, cols, 2 * len(bounds_of(cols, CFG['sizes']))),
             compiler_params=pltpu.CompilerParams(
                 collective_id=0, has_side_effects=True, vmem_limit_bytes=60 * 1024 * 1024
             ),

time: 19.6 us -> 19.6 us (level)
  no operation moved by 1% of the time
where the time goes in v9:
time: 19.6 us; the launch traced here: 19.5 us
  Pallas kernels  18.8 us (96%)
  between operations  0.64 us (3%)
    pallas_call x1, Pallas kernels, per_device(): pl.pallas_call(functools.partial(head_kernel, CFG, peers), out_shape=tupl...  18.2 us
    pallas_call x1, Pallas kernels, per_device(): pl.pallas_call(store_kernel, out_shape=tuple((jax.ShapeDtypeStruct(r.shap...  0.6 us

profile of v9, /device:TPU:21, one launch (start us, length us, event | category | flops | bytes accessed | tf_op | source)
XLA Modules:
  0.0 19.5 jit_solution(14165798256750009740)
XLA Ops:
  0.6 18.2 %shard_map.67 = (f32[2,32]{1,0:T(2,128)S(1)}, f32[3,32]{1,0:T(4,128)S(1)}, f32[3,32]{1,0:T(4,128)S(1)}) custom-call(bf16[3,32,4096]{2,1,0:T(8,128)(2,1)} %bitcast.8, s32[2,32]{1,0:T(2,128)} %bitcast.10, bf16[32,128]{1,0:T(8,128)(2,1)} %bitcast.9, bf16[2000,4096]{1,0:T(8,128)(2,1)} %bitcast.7), custom_call_target="tpu_custom_call" | custom-call | tf_op jit(solution)/shard_map/pallas_call | solution.py:232
  18.9 0.6 %shard_map.68 = (f32[2,32]{1,0:T(2,128)}, f32[3,32]{1,0:T(4,128)}, f32[3,32]{1,0:T(4,128)}) custom-call(f32[2,32]{1,0:T(2,128)S(1)} %get-tuple-element.9.refs_0_, f32[3,32]{1,0:T(4,128)S(1)} %get-tuple-element.10.refs_1_, f32[3,32]{1,0:T(4,128)S(1)} %get-tuple-element.11.refs_2_), custom_call_target="tpu_custom_call" | custom-call | tf_op jit(solution)/shard_map/pallas_call | solution.py:252

commit v10 on v9

--- a/solution.py
+++ b/solution.py
@@ -11,7 +11,7 @@
 LANES = 128
 SUBLANES = 8
 PACKED = 16
-CFG = {'sizes': (240, 320, 400, 416, 368, 256)}
+CFG = {'sizes': (160, 240, 272, 272, 272, 272, 256, 256)}
 
 
 def bounds_of(total, sizes):

time: 19.6 us -> 19.1 us (0.974)
  Pallas kernels: 18.8 us -> 18.4 us
    pallas_call x1, Pallas kernels: 18.2 us -> 17.8 us  [per_device(): pl.pallas_call(functools.partial(head_kernel, CFG, peers), out_shape=tupl...]
where the time goes in v10:
time: 19.1 us; the launch traced here: 19 us
  Pallas kernels  18.4 us (96%)
  between operations  0.64 us (3%)
    pallas_call x1, Pallas kernels, per_device(): pl.pallas_call(functools.partial(head_kernel, CFG, peers), out_shape=tupl...  17.8 us
    pallas_call x1, Pallas kernels, per_device(): pl.pallas_call(store_kernel, out_shape=tuple((jax.ShapeDtypeStruct(r.shap...  0.6 us

profile of v10, /device:TPU:21, one launch (start us, length us, event | category | flops | bytes accessed | tf_op | source)
XLA Modules:
  0.0 19.0 jit_solution(7135937116574928028)
XLA Ops:
  0.6 17.8 %shard_map.67 = (f32[2,32]{1,0:T(2,128)S(1)}, f32[3,32]{1,0:T(4,128)S(1)}, f32[3,32]{1,0:T(4,128)S(1)}) custom-call(bf16[3,32,4096]{2,1,0:T(8,128)(2,1)} %bitcast.8, s32[2,32]{1,0:T(2,128)} %bitcast.10, bf16[32,128]{1,0:T(8,128)(2,1)} %bitcast.9, bf16[2000,4096]{1,0:T(8,128)(2,1)} %bitcast.7), custom_call_target="tpu_custom_call" | custom-call | tf_op jit(solution)/shard_map/pallas_call | solution.py:232
  18.4 0.6 %shard_map.68 = (f32[2,32]{1,0:T(2,128)}, f32[3,32]{1,0:T(4,128)}, f32[3,32]{1,0:T(4,128)}) custom-call(f32[2,32]{1,0:T(2,128)S(1)} %get-tuple-element.9.refs_0_, f32[3,32]{1,0:T(4,128)S(1)} %get-tuple-element.10.refs_1_, f32[3,32]{1,0:T(4,128)S(1)} %get-tuple-element.11.refs_2_), custom_call_target="tpu_custom_call" | custom-call | tf_op jit(solution)/shard_map/pallas_call | solution.py:252

commit v11 on v10

--- a/solution.py
+++ b/solution.py
@@ -167,7 +167,7 @@
     cfg, peers,
     x_hbm, ids_hbm, gain_hbm, w_hbm,
     logp_ref, norm_ref, ent_ref,
-    own, recv, send_sem, recv_sem, *scratch,
+    own, recv, sent, send_sem, recv_sem, *scratch,
 ):
     steps, seqs, _ = scratch[0].shape
     drafts = scratch[1].shape[0]
@@ -181,33 +181,36 @@
 
     stats = local_stats(cfg, me, x_hbm, ids_hbm, gain_hbm, w_hbm, *scratch, announce)
     own[...] = stats
-    recv[:, pl.ds(me, 1), :] = stats[:, None, :]
+    slot = pl.ds(pl.multiple_of(me * SUBLANES, SUBLANES), stats.shape[0])
+    recv[slot, :] = stats
 
     pl.semaphore_wait(barrier, peers - 1)
     for target in targets:
         pltpu.make_async_remote_copy(
-            src_ref=own, dst_ref=recv.at[:, me], send_sem=send_sem, recv_sem=recv_sem,
+            src_ref=own, dst_ref=recv.at[slot], send_sem=send_sem, recv_sem=recv_sem,
             device_id={'tp': target}, device_id_type=pl.DeviceIdType.MESH,
         ).start()
-    others = recv.at[:, pl.ds(0, peers - 1)]
+    others = sent.at[pl.ds(0, peers - 1)]
     pltpu.make_async_copy(others, others, recv_sem).wait()
 
-    tops, sums, weights = (recv[i] for i in range(3))
+    tops, sums, weights = parts = [recv[pl.ds(i, peers, stride=SUBLANES), :] for i in range(3)]
+    rows = steps * seqs
+    picked = jnp.concatenate([jnp.sum(part, axis=0, keepdims=True) for part in parts[:drafts]], axis=0)[:, rows:]
     full_top = jnp.max(tops, axis=0, keepdims=True)
     drop = tops - full_top
     scale = jnp.exp(drop)
     full_sum = jnp.sum(scale * sums, axis=0, keepdims=True)
     full_weighted = jnp.sum(scale * (weights + sums * drop), axis=0, keepdims=True)
     log_sum = jnp.log(full_sum)
-    log_norm = full_top + log_sum
     entropy = log_sum - full_weighted / full_sum
-    for t in range(steps):
-        lanes = slice(t * seqs, (t + 1) * seqs)
-        norm_ref[pl.ds(t, 1), :] = log_norm[:, lanes]
-        ent_ref[pl.ds(t, 1), :] = entropy[:, lanes]
-        if t < drafts:
-            picked = jnp.sum(recv[t], axis=0, keepdims=True)[:, steps * seqs:]
-            logp_ref[pl.ds(t, 1), :] = picked - log_norm[:, lanes]
+
+    def by_step(row):
+        return jnp.concatenate([row[:, t * seqs:(t + 1) * seqs] for t in range(steps)], axis=0)
+
+    log_norm = by_step(full_top + log_sum)
+    norm_ref[...] = log_norm
+    ent_ref[...] = by_step(entropy)
+    logp_ref[...] = picked - log_norm[:drafts]
     pltpu.make_async_copy(others, others, send_sem).wait()
 
 
@@ -236,7 +239,8 @@
             out_specs=(vmem,) * 3,
             scratch_shapes=[
                 pltpu.VMEM((3, LANES), jnp.float32),
-                pltpu.VMEM((3, peers, LANES), jnp.float32),
+                pltpu.VMEM((peers * SUBLANES, LANES), jnp.float32),
+                pltpu.VMEM((peers, 3, LANES), jnp.float32),
                 pltpu.SemaphoreType.DMA,
                 pltpu.SemaphoreType.DMA,
             ] + local_scratch(steps, seqs, drafts, dim, cols, 2 * len(bounds_of(cols, CFG['sizes']))),

time: 19.1 us -> 19.2 us (level)
  no operation moved by 1% of the time
where the time goes in v11:
time: 19.2 us; the launch traced here: 19.1 us
  Pallas kernels  18.4 us (96%)
  between operations  0.64 us (3%)
    pallas_call x1, Pallas kernels, per_device(): pl.pallas_call(functools.partial(head_kernel, CFG, peers), out_shape=tupl...  17.8 us
    pallas_call x1, Pallas kernels, per_device(): pl.pallas_call(store_kernel, out_shape=tuple((jax.ShapeDtypeStruct(r.shap...  0.6 us

profile of v11, /device:TPU:21, one launch (start us, length us, event | category | flops | bytes accessed | tf_op | source)
XLA Modules:
  0.0 19.1 jit_solution(17962373601614810048)
XLA Ops:
  0.6 17.8 %shard_map.67 = (f32[2,32]{1,0:T(2,128)S(1)}, f32[3,32]{1,0:T(4,128)S(1)}, f32[3,32]{1,0:T(4,128)S(1)}) custom-call(bf16[3,32,4096]{2,1,0:T(8,128)(2,1)} %bitcast.8, s32[2,32]{1,0:T(2,128)} %bitcast.10, bf16[32,128]{1,0:T(8,128)(2,1)} %bitcast.9, bf16[2000,4096]{1,0:T(8,128)(2,1)} %bitcast.7), custom_call_target="tpu_custom_call" | custom-call | tf_op jit(solution)/shard_map/pallas_call | solution.py:235
  18.5 0.6 %shard_map.68 = (f32[2,32]{1,0:T(2,128)}, f32[3,32]{1,0:T(4,128)}, f32[3,32]{1,0:T(4,128)}) custom-call(f32[2,32]{1,0:T(2,128)S(1)} %get-tuple-element.9.refs_0_, f32[3,32]{1,0:T(4,128)S(1)} %get-tuple-element.10.refs_1_, f32[3,32]{1,0:T(4,128)S(1)} %get-tuple-element.11.refs_2_), custom_call_target="tpu_custom_call" | custom-call | tf_op jit(solution)/shard_map/pallas_call | solution.py:256

commit v12 on v11

--- a/solution.py
+++ b/solution.py
@@ -195,7 +195,11 @@
 
     tops, sums, weights = parts = [recv[pl.ds(i, peers, stride=SUBLANES), :] for i in range(3)]
     rows = steps * seqs
-    picked = jnp.concatenate([jnp.sum(part, axis=0, keepdims=True) for part in parts[:drafts]], axis=0)[:, rows:]
+    lane = lax.broadcasted_iota(jnp.int32, (1, LANES), 1)
+    picked = jnp.zeros((1, LANES), jnp.float32)
+    for t in range(drafts):
+        turned = pltpu.roll(jnp.sum(parts[t], axis=0, keepdims=True), (t * seqs - rows) % LANES, 1)
+        picked = jnp.where((lane >= t * seqs) & (lane < (t + 1) * seqs), turned, picked)
     full_top = jnp.max(tops, axis=0, keepdims=True)
     drop = tops - full_top
     scale = jnp.exp(drop)
@@ -204,13 +208,14 @@
     log_sum = jnp.log(full_sum)
     entropy = log_sum - full_weighted / full_sum
 
-    def by_step(row):
-        return jnp.concatenate([row[:, t * seqs:(t + 1) * seqs] for t in range(steps)], axis=0)
-
-    log_norm = by_step(full_top + log_sum)
-    norm_ref[...] = log_norm
-    ent_ref[...] = by_step(entropy)
-    logp_ref[...] = picked - log_norm[:drafts]
+    log_norm = full_top + log_sum
+    logp = picked - log_norm
+    for t in range(steps):
+        lanes = slice(t * seqs, (t + 1) * seqs)
+        norm_ref[pl.ds(t, 1), :] = log_norm[:, lanes]
+        ent_ref[pl.ds(t, 1), :] = entropy[:, lanes]
+        if t < drafts:
+            logp_ref[pl.ds(t, 1), :] = logp[:, lanes]
     pltpu.make_async_copy(others, others, send_sem).wait()
 
 

time: 19.2 us -> 19.1 us (level)
  no operation moved by 1% of the time
where the time goes in v12:
time: 19.1 us; the launch traced here: 19 us
  Pallas kernels  18.4 us (96%)
  between operations  0.64 us (3%)
    pallas_call x1, Pallas kernels, per_device(): pl.pallas_call(functools.partial(head_kernel, CFG, peers), out_shape=tupl...  17.8 us
    pallas_call x1, Pallas kernels, per_device(): pl.pallas_call(store_kernel, out_shape=tuple((jax.ShapeDtypeStruct(r.shap...  0.6 us

profile of v12, /device:TPU:21, one launch (start us, length us, event | category | flops | bytes accessed | tf_op | source)
XLA Modules:
  0.0 19.0 jit_solution(17807968668628939711)
XLA Ops:
  0.6 17.8 %shard_map.67 = (f32[2,32]{1,0:T(2,128)S(1)}, f32[3,32]{1,0:T(4,128)S(1)}, f32[3,32]{1,0:T(4,128)S(1)}) custom-call(bf16[3,32,4096]{2,1,0:T(8,128)(2,1)} %bitcast.8, s32[2,32]{1,0:T(2,128)} %bitcast.10, bf16[32,128]{1,0:T(8,128)(2,1)} %bitcast.9, bf16[2000,4096]{1,0:T(8,128)(2,1)} %bitcast.7), custom_call_target="tpu_custom_call" | custom-call | tf_op jit(solution)/shard_map/pallas_call | solution.py:240
  18.4 0.6 %shard_map.68 = (f32[2,32]{1,0:T(2,128)}, f32[3,32]{1,0:T(4,128)}, f32[3,32]{1,0:T(4,128)}) custom-call(f32[2,32]{1,0:T(2,128)S(1)} %get-tuple-element.9.refs_0_, f32[3,32]{1,0:T(4,128)S(1)} %get-tuple-element.10.refs_1_, f32[3,32]{1,0:T(4,128)S(1)} %get-tuple-element.11.refs_2_), custom_call_target="tpu_custom_call" | custom-call | tf_op jit(solution)/shard_map/pallas_call | solution.py:261

commit v13 on v12

--- a/solution.py
+++ b/solution.py
@@ -11,7 +11,7 @@
 LANES = 128
 SUBLANES = 8
 PACKED = 16
-CFG = {'sizes': (160, 240, 272, 272, 272, 272, 256, 256)}
+CFG = {'sizes': (256, 192, 240, 240, 192, 304, 384, 192), 'cuts': ((4, 4, 4, 4), (4, 6, 6), (4, 4, 4, 4), (6, 6, 4), (10, 6), (6, 6, 4), (4, 6, 6), (6, 10))}
 
 
 def bounds_of(total, sizes):
@@ -93,16 +93,20 @@
     gain_copy = pltpu.make_async_copy(gain_hbm, gain_vmem, small_sem.at[1])
     ids_copy = pltpu.make_async_copy(ids_hbm, ids_vmem, small_sem.at[0])
     x_copies = [pltpu.make_async_copy(x_hbm.at[t], x_vmem.at[t], x_sem.at[t]) for t in range(steps)]
-    depths = (pl.ds(0, dim // 2), pl.ds(dim // 2, dim // 2))
-    w_copies = []
-    for i, (start, size) in enumerate(chunks):
-        for depth in depths:
+    pieces, w_copies = [], []
+    for (start, size), cut in zip(chunks, cfg['cuts']):
+        edges = [dim * sum(cut[:j]) // sum(cut) for j in range(len(cut) + 1)]
+        pieces.append([pl.ds(low, high - low) for low, high in zip(edges, edges[1:])])
+        copies = []
+        for depth in pieces[-1]:
             where = (pl.ds(start, size), depth)
-            w_copies.append(pltpu.make_async_copy(w_hbm.at[where], w_vmem.at[where], w_sem.at[len(w_copies)]))
+            sem = w_sem.at[sum(len(c) for c in w_copies) + len(copies)]
+            copies.append(pltpu.make_async_copy(w_hbm.at[where], w_vmem.at[where], sem))
+        w_copies.append(copies)
     for copy in [gain_copy, ids_copy] + x_copies:
         copy.start()
     announce(0, 1)
-    for copy in w_copies:
+    for copy in sum(w_copies, []):
         copy.start()
     announce(1, None)
 
@@ -147,19 +151,24 @@
     opened = []
     for i in range(len(chunks) + 1):
         if i:
-            w_copies[2 * i - 1].wait()
+            w_copies[i - 1][-1].wait()
         if i < len(chunks):
-            w_copies[2 * i].wait()
-        closed = [(begin, part, tiles + product(begin, part, depths[1])) for begin, part, tiles in opened]
+            w_copies[i][0].wait()
+        closed = [(begin, tiles + product(begin, part, pieces[i - 1][-1])) for begin, part, tiles in opened]
         opened = []
         if i < len(chunks):
             start, size = chunks[i]
             first = -(-size // 2 // PACKED) * PACKED
+            depth = pieces[i][0].size // 2
             for begin, part in ((start, first), (start + first, size - first)):
-                low, high = (product(begin, part, pl.ds(j * (dim // 4), dim // 4)) for j in range(2))
+                low, high = (product(begin, part, pl.ds(j * depth, depth)) for j in range(2))
                 opened.append((begin, part, low + high))
-        for begin, _, tiles in closed:
+        for begin, tiles in closed:
             carry = stats_of(carry, local_ids, begin, tiles)
+        if i < len(chunks):
+            for copy, piece in zip(w_copies[i][1:-1], pieces[i][1:-1]):
+                copy.wait()
+                opened = [(begin, part, tiles + product(begin, part, piece)) for begin, part, tiles in opened]
     return fold(carry, steps * seqs, drafts)
 
 
@@ -248,7 +257,7 @@
                 pltpu.VMEM((peers, 3, LANES), jnp.float32),
                 pltpu.SemaphoreType.DMA,
                 pltpu.SemaphoreType.DMA,
-            ] + local_scratch(steps, seqs, drafts, dim, cols, 2 * len(bounds_of(cols, CFG['sizes']))),
+            ] + local_scratch(steps, seqs, drafts, dim, cols, sum(len(cut) for cut in CFG['cuts'])),
             compiler_params=pltpu.CompilerParams(
                 collective_id=0, has_side_effects=True, vmem_limit_bytes=60 * 1024 * 1024
             ),

time: 19.1 us -> 19.2 us (level)
  no operation moved by 1% of the time
where the time goes in v13:
time: 19.2 us; the launch traced here: 19.1 us
  Pallas kernels  18.5 us (96%)
  between operations  0.64 us (3%)
    pallas_call x1, Pallas kernels, per_device(): pl.pallas_call(functools.partial(head_kernel, CFG, peers), out_shape=tupl...  17.9 us
    pallas_call x1, Pallas kernels, per_device(): pl.pallas_call(store_kernel, out_shape=tuple((jax.ShapeDtypeStruct(r.shap...  0.6 us

profile of v13, /device:TPU:21, one launch (start us, length us, event | category | flops | bytes accessed | tf_op | source)
XLA Modules:
  0.0 19.1 jit_solution(8807112402358298228)
XLA Ops:
  0.6 17.9 %shard_map.67 = (f32[2,32]{1,0:T(2,128)S(1)}, f32[3,32]{1,0:T(4,128)S(1)}, f32[3,32]{1,0:T(4,128)S(1)}) custom-call(bf16[3,32,4096]{2,1,0:T(8,128)(2,1)} %bitcast.8, s32[2,32]{1,0:T(2,128)} %bitcast.10, bf16[32,128]{1,0:T(8,128)(2,1)} %bitcast.9, bf16[2000,4096]{1,0:T(8,128)(2,1)} %bitcast.7), custom_call_target="tpu_custom_call" | custom-call | tf_op jit(solution)/shard_map/pallas_call | solution.py:249
  18.5 0.6 %shard_map.68 = (f32[2,32]{1,0:T(2,128)}, f32[3,32]{1,0:T(4,128)}, f32[3,32]{1,0:T(4,128)}) custom-call(f32[2,32]{1,0:T(2,128)S(1)} %get-tuple-element.9.refs_0_, f32[3,32]{1,0:T(4,128)S(1)} %get-tuple-element.10.refs_1_, f32[3,32]{1,0:T(4,128)S(1)} %get-tuple-element.11.refs_2_), custom_call_target="tpu_custom_call" | custom-call | tf_op jit(solution)/shard_map/pallas_call | solution.py:270

commit v14 on v12

--- a/solution.py
+++ b/solution.py
@@ -11,7 +11,7 @@
 LANES = 128
 SUBLANES = 8
 PACKED = 16
-CFG = {'sizes': (160, 240, 272, 272, 272, 272, 256, 256)}
+CFG = {'sizes': (224, 192, 192, 208, 224, 224, 256, 288, 192)}
 
 
 def bounds_of(total, sizes):

time: 19.1 us -> 19.2 us (level)
  no operation moved by 1% of the time
where the time goes in v14:
time: 19.2 us; the launch traced here: 19.1 us
  Pallas kernels  18.4 us (96%)
  between operations  0.64 us (3%)
    pallas_call x1, Pallas kernels, per_device(): pl.pallas_call(functools.partial(head_kernel, CFG, peers), out_shape=tupl...  17.8 us
    pallas_call x1, Pallas kernels, per_device(): pl.pallas_call(store_kernel, out_shape=tuple((jax.ShapeDtypeStruct(r.shap...  0.6 us

profile of v14, /device:TPU:21, one launch (start us, length us, event | category | flops | bytes accessed | tf_op | source)
XLA Modules:
  0.0 19.1 jit_solution(15638973761798976902)
XLA Ops:
  0.6 17.8 %shard_map.67 = (f32[2,32]{1,0:T(2,128)S(1)}, f32[3,32]{1,0:T(4,128)S(1)}, f32[3,32]{1,0:T(4,128)S(1)}) custom-call(bf16[3,32,4096]{2,1,0:T(8,128)(2,1)} %bitcast.8, s32[2,32]{1,0:T(2,128)} %bitcast.10, bf16[32,128]{1,0:T(8,128)(2,1)} %bitcast.9, bf16[2000,4096]{1,0:T(8,128)(2,1)} %bitcast.7), custom_call_target="tpu_custom_call" | custom-call | tf_op jit(solution)/shard_map/pallas_call | solution.py:240
  18.5 0.6 %shard_map.68 = (f32[2,32]{1,0:T(2,128)}, f32[3,32]{1,0:T(4,128)}, f32[3,32]{1,0:T(4,128)}) custom-call(f32[2,32]{1,0:T(2,128)S(1)} %get-tuple-element.9.refs_0_, f32[3,32]{1,0:T(4,128)S(1)} %get-tuple-element.10.refs_1_, f32[3,32]{1,0:T(4,128)S(1)} %get-tuple-element.11.refs_2_), custom_call_target="tpu_custom_call" | custom-call | tf_op jit(solution)/shard_map/pallas_call | solution.py:261

commit v15 on v14

--- a/solution.py
+++ b/solution.py
@@ -11,7 +11,7 @@
 LANES = 128
 SUBLANES = 8
 PACKED = 16
-CFG = {'sizes': (224, 192, 192, 208, 224, 224, 256, 288, 192)}
+CFG = {'sizes': (144, 224, 272, 288, 288, 288, 272, 224)}
 
 
 def bounds_of(total, sizes):

time: 19.2 us -> 19.1 us (level)
  no operation moved by 1% of the time
where the time goes in v15:
time: 19.1 us
  Pallas kernels  18.4 us (96%)
  between operations  0.64 us (3%)
    pallas_call x1, Pallas kernels, per_device(): pl.pallas_call(functools.partial(head_kernel, CFG, peers), out_shape=tupl...  17.8 us
    pallas_call x1, Pallas kernels, per_device(): pl.pallas_call(store_kernel, out_shape=tuple((jax.ShapeDtypeStruct(r.shap...  0.6 us

profile of v15, /device:TPU:21, one launch (start us, length us, event | category | flops | bytes accessed | tf_op | source)
XLA Modules:
  0.0 19.1 jit_solution(10069125838757864857)
XLA Ops:
  0.6 17.8 %shard_map.67 = (f32[2,32]{1,0:T(2,128)S(1)}, f32[3,32]{1,0:T(4,128)S(1)}, f32[3,32]{1,0:T(4,128)S(1)}) custom-call(bf16[3,32,4096]{2,1,0:T(8,128)(2,1)} %bitcast.8, s32[2,32]{1,0:T(2,128)} %bitcast.10, bf16[32,128]{1,0:T(8,128)(2,1)} %bitcast.9, bf16[2000,4096]{1,0:T(8,128)(2,1)} %bitcast.7), custom_call_target="tpu_custom_call" | custom-call | tf_op jit(solution)/shard_map/pallas_call | solution.py:240
  18.5 0.6 %shard_map.68 = (f32[2,32]{1,0:T(2,128)}, f32[3,32]{1,0:T(4,128)}, f32[3,32]{1,0:T(4,128)}) custom-call(f32[2,32]{1,0:T(2,128)S(1)} %get-tuple-element.9.refs_0_, f32[3,32]{1,0:T(4,128)S(1)} %get-tuple-element.10.refs_1_, f32[3,32]{1,0:T(4,128)S(1)} %get-tuple-element.11.refs_2_), custom_call_target="tpu_custom_call" | custom-call | tf_op jit(solution)/shard_map/pallas_call | solution.py:261

commit v16 on v15

--- a/solution.py
+++ b/solution.py
@@ -11,7 +11,7 @@
 LANES = 128
 SUBLANES = 8
 PACKED = 16
-CFG = {'sizes': (144, 224, 272, 288, 288, 288, 272, 224)}
+CFG = {'sizes': (160, 256, 272, 272, 272, 272, 272, 224)}
 
 
 def bounds_of(total, sizes):

time: 19.1 us -> 19.1 us (level)
  no operation moved by 1% of the time
where the time goes in v16:
time: 19.1 us; the launch traced here: 19 us
  Pallas kernels  18.4 us (96%)
  between operations  0.64 us (3%)
    pallas_call x1, Pallas kernels, per_device(): pl.pallas_call(functools.partial(head_kernel, CFG, peers), out_shape=tupl...  17.8 us
    pallas_call x1, Pallas kernels, per_device(): pl.pallas_call(store_kernel, out_shape=tuple((jax.ShapeDtypeStruct(r.shap...  0.6 us

profile of v16, /device:TPU:21, one launch (start us, length us, event | category | flops | bytes accessed | tf_op | source)
XLA Modules:
  0.0 19.0 jit_solution(16261120334591187330)
XLA Ops:
  0.6 17.8 %shard_map.67 = (f32[2,32]{1,0:T(2,128)S(1)}, f32[3,32]{1,0:T(4,128)S(1)}, f32[3,32]{1,0:T(4,128)S(1)}) custom-call(bf16[3,32,4096]{2,1,0:T(8,128)(2,1)} %bitcast.8, s32[2,32]{1,0:T(2,128)} %bitcast.10, bf16[32,128]{1,0:T(8,128)(2,1)} %bitcast.9, bf16[2000,4096]{1,0:T(8,128)(2,1)} %bitcast.7), custom_call_target="tpu_custom_call" | custom-call | tf_op jit(solution)/shard_map/pallas_call | solution.py:240
  18.4 0.6 %shard_map.68 = (f32[2,32]{1,0:T(2,128)}, f32[3,32]{1,0:T(4,128)}, f32[3,32]{1,0:T(4,128)}) custom-call(f32[2,32]{1,0:T(2,128)S(1)} %get-tuple-element.9.refs_0_, f32[3,32]{1,0:T(4,128)S(1)} %get-tuple-element.10.refs_1_, f32[3,32]{1,0:T(4,128)S(1)} %get-tuple-element.11.refs_2_), custom_call_target="tpu_custom_call" | custom-call | tf_op jit(solution)/shard_map/pallas_call | solution.py:261

commit v17 on v16

--- a/solution.py
+++ b/solution.py
@@ -11,7 +11,7 @@
 LANES = 128
 SUBLANES = 8
 PACKED = 16
-CFG = {'sizes': (160, 256, 272, 272, 272, 272, 272, 224)}
+CFG = {'sizes': (160, 240, 256, 272, 272, 272, 272, 256)}
 
 
 def bounds_of(total, sizes):

time: 19.1 us -> 19.1 us (level)
  no operation moved by 1% of the time
where the time goes in v17:
time: 19.1 us; the launch traced here: 19 us
  Pallas kernels  18.4 us (96%)
  between operations  0.64 us (3%)
    pallas_call x1, Pallas kernels, per_device(): pl.pallas_call(functools.partial(head_kernel, CFG, peers), out_shape=tupl...  17.8 us
    pallas_call x1, Pallas kernels, per_device(): pl.pallas_call(store_kernel, out_shape=tuple((jax.ShapeDtypeStruct(r.shap...  0.6 us

profile of v17, /device:TPU:21, one launch (start us, length us, event | category | flops | bytes accessed | tf_op | source)
XLA Modules:
  0.0 19.0 jit_solution(9452657677818502327)
XLA Ops:
  0.6 17.8 %shard_map.67 = (f32[2,32]{1,0:T(2,128)S(1)}, f32[3,32]{1,0:T(4,128)S(1)}, f32[3,32]{1,0:T(4,128)S(1)}) custom-call(bf16[3,32,4096]{2,1,0:T(8,128)(2,1)} %bitcast.8, s32[2,32]{1,0:T(2,128)} %bitcast.10, bf16[32,128]{1,0:T(8,128)(2,1)} %bitcast.9, bf16[2000,4096]{1,0:T(8,128)(2,1)} %bitcast.7), custom_call_target="tpu_custom_call" | custom-call | tf_op jit(solution)/shard_map/pallas_call | solution.py:240
  18.4 0.6 %shard_map.68 = (f32[2,32]{1,0:T(2,128)}, f32[3,32]{1,0:T(4,128)}, f32[3,32]{1,0:T(4,128)}) custom-call(f32[2,32]{1,0:T(2,128)S(1)} %get-tuple-element.9.refs_0_, f32[3,32]{1,0:T(4,128)S(1)} %get-tuple-element.10.refs_1_, f32[3,32]{1,0:T(4,128)S(1)} %get-tuple-element.11.refs_2_), custom_call_target="tpu_custom_call" | custom-call | tf_op jit(solution)/shard_map/pallas_call | solution.py:261
